TPU v7x, 256 devices: a whole 4x4x8 slice. The times are simulated.
256 devices in a mesh: prow: 16 (over x_hi, z), pcol: 16 (over x_lo, y, core).
Axes of the slice: x: 4 (x_hi: 2, x_lo: 2; x = x_hi * 2 + x_lo), y: 4, z: 8, core: 2. Of those that a mesh axis runs over, the one named last changes fastest.
Arguments:
- system: bfloat16 [12288, 65536], P('prow', 'pcol'), may hold values from -6 to 6
- row_outer: float32 [12288], P('prow'), may hold values from 0.5 to 2
- row_inner: float32 [12288], P('prow'), may hold values from 0.5 to 2
- col_outer: float32 [65536], P('pcol'), may hold values from 0.5 to 2
- col_inner: float32 [65536], P('pcol'), may hold values from 0.5 to 2
- diag_inverse: bfloat16 [512, 512], replicated, may hold values from -0.01171875 to 0.01171875
Outputs:
- trailing: bfloat16 [12288, 65536], P('prow', 'pcol')
All inputs are finite; a program needn't handle non-finite values.
Results may differ from a plain program's by a relative error of at most 0.0089.
Values may be sent and summed in bfloat16 or wider, within the bound.
No kernel may reach another device: no remote copies, remote signals or barrier semaphores. Data moves between devices by JAX's collectives and lax.ppermute only.
A program may use at most 192 MiB of HBM per device.

v0:
```python
import jax
import jax.numpy as jnp
from jax import lax
from jax.sharding import PartitionSpec as P

root_half = 0.7071067811865476


def partner_2(block, axis, stride):
    count = lax.axis_size(axis)
    route = []
    for low in range(count):
        high = low | 1 << stride
        if high != low and high < count:
            route += [(low, high), (high, low)]
    return lax.ppermute(block, axis, route)


def picked(x, axis, root):
    return lax.dynamic_index_in_dim(lax.all_gather(x, axis), root, 0, keepdims=False)


def combine(values, partner, weights, upper):
    mine = values.astype(jnp.float32)
    other = partner.astype(jnp.float32)
    summed = jnp.where(upper, mine + other, other - mine)
    return (weights * summed * root_half).astype(jnp.bfloat16)


def per_device(system, row_outer, row_inner, col_outer, col_inner, diag_inverse):
    panel = diag_inverse.shape[0]
    rows_here = system.shape[0]
    row_bits = lax.axis_size("prow").bit_length() - 1
    col_bits = lax.axis_size("pcol").bit_length() - 1
    row_place = lax.axis_index("prow")
    col_place = lax.axis_index("pcol")
    partner = partner_2(system, "prow", row_bits - 1)
    first = combine(system, partner, row_outer[:, None], row_place >> row_bits - 1 & 1 == 0)
    partner = partner_2(first, "prow", row_bits - 2)
    second = combine(first, partner, row_inner[:, None], row_place >> row_bits - 2 & 1 == 0)
    partner = partner_2(second, "pcol", col_bits - 1)
    third = combine(second, partner, col_outer[None, :], col_place >> col_bits - 1 & 1 == 0)
    partner = partner_2(third, "pcol", col_bits - 2)
    transformed = combine(third, partner, col_inner[None, :], col_place >> col_bits - 2 & 1 == 0)
    leading = transformed[:, :panel]
    factor = jnp.dot(leading, diag_inverse, preferred_element_type=jnp.float32).astype(jnp.bfloat16)
    left = picked(factor, "pcol", 0)
    taken = min(rows_here, panel)
    piece = transformed[:taken].astype(jnp.float32)
    term = piece * (row_place == 0).astype(jnp.float32)
    top_rows = lax.psum(term.astype(jnp.bfloat16), "prow")
    update = jnp.dot(left, top_rows, preferred_element_type=jnp.float32)
    return (transformed.astype(jnp.float32) - update).astype(jnp.bfloat16)


def solution(mesh):
    in_specs = (P("prow", "pcol"), P("prow"), P("prow"), P("pcol"), P("pcol"), P())
    out_specs = P("prow", "pcol")
    return jax.shard_map(
        per_device, mesh=mesh, in_specs=in_specs, out_specs=out_specs, check_vma=False
    )
```

profile of v0, /device:TPU:24, one launch (start us, length us, event | category | flops | bytes accessed | tf_op | source)
XLA Modules:
  0.0 931.7 jit_solution(14636197463177600740)
XLA Ops:
  7.4 0.0 copy-start
  7.4 0.0 copy-start.4
  7.4 0.0 all-reduce.2.cloned.1.call-start
  7.4 3.0 collective-permute-start
  10.4 136.0 %collective-permute-done = bf16[768,4096]{1,0:T(8,128)(2,1)} collective-permute-done((bf16[768,4096]{1,0:T(8,128)(2,1)}, bf16[768,4096]{1,0:T(8,128)(2,1)}, u32[]{:S(2)}, u32[]{:S(2)}) %collective-permute-start) | collective-permute-done | bytes 6291488 | tf_op jit(solution)/shard_map/ppermute | solution.py:16
  146.4 9.5 %fusion.3 = bf16[768,4096]{1,0:T(8,128)(2,1)} fusion(bf16[768,4096]{1,0:T(8,128)(2,1)} %collective-permute-done, bf16[768,4096]{1,0:T(8,128)(2,1)} %param.6, f32[768]{0:T(1024)} %param.7, pred[]{:T(512)S(6)} %eq.18), kind=kLoop, calls=%fused_computation.11 | loop fusion | flops 25165824 | bytes 18877440 | tf_op jit(solution)/shard_map/convert_element_type | solution.py:27
  156.0 0.0 copy-start.2
  156.0 7.2 collective-permute-start.1
  163.2 272.1 %collective-permute-done.1 = bf16[768,4096]{1,0:T(8,128)(2,1)} collective-permute-done((bf16[768,4096]{1,0:T(8,128)(2,1)}, bf16[768,4096]{1,0:T(8,128)(2,1)}, u32[]{:S(2)}, u32[]{:S(2)}) %collective-permute-start.1) | collective-permute-done | bytes 6291488 | tf_op jit(solution)/shard_map/ppermute | solution.py:16
  435.2 0.0 copy-done.4
  435.2 9.6 %fusion.7 = bf16[768,4096]{1,0:T(8,128)(2,1)} fusion(bf16[768,4096]{1,0:T(8,128)(2,1)} %collective-permute-done.1, bf16[768,4096]{1,0:T(8,128)(2,1)} %fusion.3, f32[768]{0:T(1024)S(1)} %copy-done.4, pred[]{:T(512)S(6)} %eq.17), kind=kLoop, calls=%fused_computation.15 | loop fusion | flops 25165824 | bytes 18877440 | tf_op jit(solution)/shard_map/convert_element_type | solution.py:27
  444.8 0.0 copy-start.3
  444.8 1.5 collective-permute-start.2
  446.3 132.9 %collective-permute-done.2 = bf16[768,4096]{1,0:T(8,128)(2,1)} collective-permute-done((bf16[768,4096]{1,0:T(8,128)(2,1)}, bf16[768,4096]{1,0:T(8,128)(2,1)}, u32[]{:S(2)}, u32[]{:S(2)}) %collective-permute-start.2) | collective-permute-done | bytes 6291488 | tf_op jit(solution)/shard_map/ppermute | solution.py:16
  579.2 0.0 copy-done.2
  579.2 9.4 %fusion.11 = bf16[768,4096]{1,0:T(8,128)(2,1)} fusion(bf16[768,4096]{1,0:T(8,128)(2,1)} %collective-permute-done.2, bf16[768,4096]{1,0:T(8,128)(2,1)} %fusion.7, f32[4096]{0:T(1024)S(1)} %copy-done.2, pred[]{:T(512)S(6)} %eq.16), kind=kLoop, calls=%fused_computation.19 | loop fusion | flops 25165824 | bytes 18890752 | tf_op jit(solution)/shard_map/convert_element_type | solution.py:27
  588.6 1.2 collective-permute-start.3
  589.8 133.8 %collective-permute-done.3 = bf16[768,4096]{1,0:T(8,128)(2,1)} collective-permute-done((bf16[768,4096]{1,0:T(8,128)(2,1)}, bf16[768,4096]{1,0:T(8,128)(2,1)}, u32[]{:S(2)}, u32[]{:S(2)}) %collective-permute-start.3) | collective-permute-done | bytes 6291488 | tf_op jit(solution)/shard_map/ppermute | solution.py:16
  723.6 0.0 copy-done.3
  723.6 6.6 fusion.15
  730.2 0.0 copy-start.1
  730.2 2.7 copy-done.1
  732.9 2.8 multiply_convert_fusion
  735.7 0.0 all-reduce.2.cloned.1.call-update
  735.7 0.0 all-gather.3.cloned.1.call-start
  735.7 0.0 copy-done
  735.8 2.6 convolution_convert_fusion
  738.4 0.0 all-gather.3.cloned.1.call-update
  738.4 175.5 %all-reduce.2.cloned.1.call-done = bf16[512,4096]{1,0:T(8,128)(2,1)} async-done(((bf16[512,4096]{1,0:T(8,128)(2,1)}), bf16[512,4096]{1,0:T(8,128)(2,1)}) %all-reduce.2.cloned.1.call-update) | async-done | bytes 4194320 | tf_op jit(solution)/shard_map/psum | solution.py:51
  913.9 0.0 all-gather.3.cloned.1.call-done
  913.9 10.4 %subtract_convert_fusion = bf16[768,4096]{1,0:T(8,128)(2,1)} fusion(bf16[768,4096]{1,0:T(8,128)(2,1)} %copy-done.1, bf16[512,4096]{1,0:T(8,128)(2,1)} %all-reduce.2.cloned.1.call-done, bf16[12288,512]{1,0:T(8,128)(2,1)} %all-gather.3.cloned.1.call-done), kind=kOutput, calls=%fused_computation.24 | convolution fusion | flops 3230662656 | bytes 17563648 | tf_op jit(solution)/shard_map/dot_general | solution.py:52
Async XLA Ops:
  7.4 728.4 %copy-start = (bf16[512,512]{1,0:T(8,128)(2,1)S(1)}, bf16[512,512]{1,0:T(8,128)(2,1)}, u32[]{:S(2)}) copy-start(bf16[512,512]{1,0:T(8,128)(2,1)} %param.11) | copy-start | bytes 1572868
  7.4 427.9 %copy-start.4 = (f32[768]{0:T(1024)S(1)}, f32[768]{0:T(1024)}, u32[]{:S(2)}) copy-start(f32[768]{0:T(1024)} %param.8) | copy-start | bytes 9220
  7.4 906.5 %all-reduce.2.cloned.1.call-start = ((), (), s32[]{:S(2)}) async-start(), calls=%async_computation | async-start | bytes 8388608 | tf_op jit(solution)/shard_map/psum | solution.py:51
  7.4 139.1 %collective-permute-start = (bf16[768,4096]{1,0:T(8,128)(2,1)}, bf16[768,4096]{1,0:T(8,128)(2,1)}, u32[]{:S(2)}, u32[]{:S(2)}) collective-permute-start(bf16[768,4096]{1,0:T(8,128)(2,1)} %param.6), channel_id=1, source_target_pairs={{0,128},{128,0},{16,144},{144,16},{32,160},{160,32},{48,176},{176,... | collective-permute-start | bytes 18874376 | tf_op jit(solution)/shard_map/ppermute | solution.py:16
  156.0 423.2 %copy-start.2 = (f32[4096]{0:T(1024)S(1)}, f32[4096]{0:T(1024)}, u32[]{:S(2)}) copy-start(f32[4096]{0:T(1024)} %param.9) | copy-start | bytes 49156
  156.0 279.2 %collective-permute-start.1 = (bf16[768,4096]{1,0:T(8,128)(2,1)}, bf16[768,4096]{1,0:T(8,128)(2,1)}, u32[]{:S(2)}, u32[]{:S(2)}) collective-permute-start(bf16[768,4096]{1,0:T(8,128)(2,1)} %fusion.3), channel_id=1, source_target_pairs={{0,64},{64,0},{16,80},{80,16},{32,96},{96,32},{48,112},{112,48},{1... | collective-permute-start | bytes 18874376 | tf_op jit(solution)/shard_map/ppermute | solution.py:16
  444.8 278.8 %copy-start.3 = (f32[4096]{0:T(1024)S(1)}, f32[4096]{0:T(1024)}, u32[]{:S(2)}) copy-start(f32[4096]{0:T(1024)} %param.10) | copy-start | bytes 49156
  444.8 134.4 %collective-permute-start.2 = (bf16[768,4096]{1,0:T(8,128)(2,1)}, bf16[768,4096]{1,0:T(8,128)(2,1)}, u32[]{:S(2)}, u32[]{:S(2)}) collective-permute-start(bf16[768,4096]{1,0:T(8,128)(2,1)} %fusion.7), channel_id=1, source_target_pairs={{0,8},{8,0},{1,9},{9,1},{2,10},{10,2},{3,11},{11,3},{4,12},{12,4},... | collective-permute-start | bytes 18874376 | tf_op jit(solution)/shard_map/ppermute | solution.py:16
  588.6 135.0 %collective-permute-start.3 = (bf16[768,4096]{1,0:T(8,128)(2,1)}, bf16[768,4096]{1,0:T(8,128)(2,1)}, u32[]{:S(2)}, u32[]{:S(2)}) collective-permute-start(bf16[768,4096]{1,0:T(8,128)(2,1)} %fusion.11), channel_id=1, source_target_pairs={{0,4},{4,0},{1,5},{5,1},{2,6},{6,2},{3,7},{7,3},{8,12},{12,8},{9,1... | collective-permute-start | bytes 18874376 | tf_op jit(solution)/shard_map/ppermute | solution.py:16
  730.2 2.7 copy-start.1
  735.7 178.2 %all-gather.3.cloned.1.call-start = ((), (), s32[]{:S(2)}) async-start(), calls=%async_computation.1 | async-start | bytes 13369344 | tf_op jit(solution)/shard_map/all_gather | solution.py:20
Sparse Core Ops, SparseCore 0:
  735.8 178.0 all-reduce.1
Sparse Core Ops, SparseCore 1:
  738.5 146.5 all-gather.2
where the time goes:
time: 932 us
  waiting for transfers between devices  850 us (91%)
  other arithmetic  37.8 us (4%)
  between operations  14.9 us (2%)
  starting transfers between devices  13 us (1%)
  matrix products  13 us (1%)
    ppermute x4, waiting for transfers between devices, partner_2(): return lax.ppermute(block, axis, route)  675 us
    psum x1, waiting for transfers between devices, per_device(): top_rows = lax.psum(term.astype(jnp.bfloat16), 'prow')  175 us
    convert_element_type x4, other arithmetic, combine(): return (weights * summed * root_half).astype(jnp.bfloat16)  35 us
  transfers between devices with their start and end apart: 6, of which 5 were waited for; matrix products, arithmetic and copies ran while one was open for 0% of the time, Pallas kernels for 0%

commit v1 on v0

v1 whole, which is shorter than its diff:
```python
import functools
import jax
import jax.numpy as jnp
from jax import lax
from jax.experimental import pallas as pl
from jax.experimental.pallas import tpu as pltpu
from jax.sharding import Mesh, PartitionSpec as P

root_half = 0.7071067811865476
f32, bf16 = jnp.float32, jnp.bfloat16
X4 = ("xh", "xl")
Y4 = ("yh", "yl")


def rows_of(total):
    for tile in (192, 96, 64, 48, 32, 16, 8):
        if total % tile == 0:
            return tile
    return total


def sub_rows(tile):
    return 16 if tile % 16 == 0 else 8


def call(body, grid, ins, outs, shapes, flops, nbytes, aliases=None, name=None):
    return pl.pallas_call(
        body,
        grid_spec=pltpu.PrefetchScalarGridSpec(
            num_scalar_prefetch=1, grid=grid, in_specs=ins, out_specs=outs
        ),
        out_shape=shapes,
        input_output_aliases=aliases or {},
        cost_estimate=pl.CostEstimate(flops=flops, bytes_accessed=nbytes, transcendentals=0),
        compiler_params=pltpu.CompilerParams(vmem_limit_bytes=8 * 1024 * 1024),
        name=name,
    )


def split_body(n, s, *refs):
    ins, outs = refs[:6], refs[6:]
    for e in range(3):
        outs[e][0] = ins[e][...]
        outs[e][1] = ins[3 + e][...]


def split_slices(scalars, system, other, width):
    rows = system.shape[0]
    tile = rows_of(rows)
    own = [pl.BlockSpec((tile, width), lambda i, s, e=e: (i, s[4 + e])) for e in (1, 2, 3)]
    got = [pl.BlockSpec((tile, width), lambda i, s, e=e: (i, s[e])) for e in (1, 2, 3)]
    out = [pl.BlockSpec((2, tile, width), lambda i, s: (0, i, 0))] * 3
    shape = [jax.ShapeDtypeStruct((2, rows, width), bf16)] * 3
    size = 3 * 2 * rows * width
    return call(functools.partial(split_body, 0), (rows // tile,), own + got, out, shape, size, 4 * size, name="split")(
        scalars, *([system] * 3), *([other] * 3)
    )


def rounded(v):
    return v.astype(bf16).astype(f32)


def mix_body(step, s, own, got, r1, r2, r3, wrow, wcol, out):
    count = own.shape[0] // step

    @pl.loop(0, count)
    def _(t):
        at = pl.ds(pl.multiple_of(t * step, step), step)
        w = wrow[at, :]
        lows, highs = [], []
        for ez in range(2):
            mine = (own if ez == 0 else got)[at, :].astype(f32)
            p = [[mine, r1[ez, at, :].astype(f32)], [r2[ez, at, :].astype(f32), r3[ez, at, :].astype(f32)]]
            lows.append([rounded((p[0][el] + p[1][el]) * w[:, ez : ez + 1]) for el in range(2)])
            highs.append([rounded((p[0][el] - p[1][el]) * w[:, 2 + ez : 3 + ez]) for el in range(2)])
        for xh, f in enumerate((lows, highs)):
            for zh in range(2):
                scale = w[:, 4 + 2 * xh + zh : 5 + 2 * xh + zh]
                g = [rounded((f[0][el] + f[1][el] if zh == 0 else f[0][el] - f[1][el]) * scale) for el in range(2)]
                out[2 * xh, zh, at, :] = ((g[0] + g[1]) * wcol[0:1, :]).astype(bf16)
                out[2 * xh + 1, zh, at, :] = ((g[0] - g[1]) * wcol[1:2, :]).astype(bf16)


def mix(scalars, system, other, received, wrow, wcol):
    rows = system.shape[0]
    width = wcol.shape[1]
    tile = rows_of(rows)
    ins = [
        pl.BlockSpec((tile, width), lambda i, s: (i, s[4])),
        pl.BlockSpec((tile, width), lambda i, s: (i, s[0])),
        *[pl.BlockSpec((2, tile, width), lambda i, s: (0, i, 0))] * 3,
        pl.BlockSpec((tile, 8), lambda i, s: (i, 0)),
        pl.BlockSpec((8, width), lambda i, s: (0, 0)),
    ]
    out = pl.BlockSpec((4, 2, tile, width), lambda i, s: (0, 0, i, 0))
    shape = jax.ShapeDtypeStruct((4, 2, rows, width), bf16)
    size = 8 * rows * width
    return call(
        functools.partial(mix_body, sub_rows(tile)), (rows // tile,), ins, out, shape, 8 * size, 4 * size, name="mix"
    )(scalars, system, other, *received, wrow, wcol)


def inner_body(step, s, mine, partner, wcol, out):
    count = mine.shape[2] // step

    @pl.loop(0, count)
    def _(t):
        at = pl.ds(pl.multiple_of(t * step, step), step)
        for x in range(4):
            for zh in range(2):
                v = mine[x, zh, at, :].astype(f32) * wcol[4:5, :] + partner[x, zh, at, :].astype(f32)
                out[x, zh, at, :] = (v * wcol[2 + x % 2 : 3 + x % 2, :]).astype(bf16)


def inner(scalars, mine, partner, wcol):
    _, _, rows, width = mine.shape
    tile = rows_of(rows)
    big = pl.BlockSpec((4, 2, tile, width), lambda i, s: (0, 0, i, 0))
    size = 8 * rows * width
    return call(
        functools.partial(inner_body, sub_rows(tile)),
        (rows // tile,),
        [big, big, pl.BlockSpec((8, width), lambda i, s: (0, 0))],
        big,
        jax.ShapeDtypeStruct(mine.shape, bf16),
        4 * size,
        6 * size,
        name="inner",
    )(scalars, mine, partner, wcol)


def factor_body(s, p0, p1, p2, p3, dinv, out):
    width = p0.shape[-1]
    for a in range(2):
        for b in range(2):
            acc = None
            for e, p in enumerate((p0, p1, p2, p3)):
                at = pl.ds(pl.multiple_of(s[e] * width, width), width)
                d = jnp.dot(p[a, b], dinv[at, :], preferred_element_type=f32)
                acc = d if acc is None else acc + d
            out[a, b] = acc.astype(bf16)


def factor(scalars, pieces, dinv):
    _, _, rows, width = pieces[0].shape
    panel = dinv.shape[0]
    tile = rows_of(rows)
    return call(
        factor_body,
        (rows // tile,),
        [pl.BlockSpec((2, 2, tile, width), lambda i, s: (0, 0, i, 0))] * 4
        + [pl.BlockSpec((panel, panel), lambda i, s: (0, 0))],
        pl.BlockSpec((2, 2, tile, panel), lambda i, s: (0, 0, i, 0)),
        jax.ShapeDtypeStruct((2, 2, rows, panel), bf16),
        8 * rows * panel * panel,
        16 * rows * panel,
        name="factor",
    )(scalars, *pieces, dinv)


def update_body(s, full, left, top, *outs):
    for e in range(4):
        x = s[e]
        for zh in range(2):
            d = jnp.dot(left[x // 2, zh], top[x % 2], preferred_element_type=f32)
            outs[e][zh] = (full[x, zh].astype(f32) - d).astype(bf16)


def update(scalars, full, left, top):
    _, _, rows, width = full.shape
    panel = left.shape[-1]
    tile = rows_of(rows)
    out = pl.BlockSpec((2, tile, width), lambda i, s: (0, i, 0))
    size = 8 * rows * width
    return call(
        update_body,
        (rows // tile,),
        [
            pl.BlockSpec((4, 2, tile, width), lambda i, s: (0, 0, i, 0)),
            pl.BlockSpec((2, 2, tile, panel), lambda i, s: (0, 0, i, 0)),
            pl.BlockSpec((2, panel, width), lambda i, s: (0, 0, 0)),
        ],
        [out] * 4,
        [jax.ShapeDtypeStruct((2, rows, width), bf16)] * 4,
        2 * size * panel,
        4 * size + 8 * rows * panel,
        name="update",
    )(scalars, full, left, top)


def gather_body(s, p0, p1, p2, p3, keep, send):
    width = p0.shape[-1]
    zh = s[8]
    for e, p in enumerate((p0, p1, p2, p3)):
        at = pl.ds(pl.multiple_of(s[e] * width, width), width)
        keep[:, at] = p[zh]
        send[:, at] = p[1 - zh]


def gather_slices(scalars, pieces):
    _, rows, width = pieces[0].shape
    tile = rows_of(rows)
    out = pl.BlockSpec((tile, 4 * width), lambda i, s: (i, 0))
    size = 8 * rows * width
    return call(
        gather_body,
        (rows // tile,),
        [pl.BlockSpec((2, tile, width), lambda i, s: (0, i, 0))] * 4,
        [out] * 2,
        [jax.ShapeDtypeStruct((rows, 4 * width), bf16)] * 2,
        size,
        4 * size,
        name="gather",
    )(scalars, *pieces)


def place_body(s, keep, got, *refs):
    out = refs[-1]
    half = keep.shape[1]
    zh = s[8]
    out[:, pl.ds(pl.multiple_of(zh * half, half), half)] = keep[...]
    out[:, pl.ds(pl.multiple_of((1 - zh) * half, half), half)] = got[...]


def place(scalars, keep, got, whole, k, columns):
    rows, half = keep.shape
    tile = rows_of(rows)
    piece = pl.BlockSpec((tile, half), lambda i, s: (i, 0))
    ins, args, aliases = [piece, piece], [keep, got], {}
    if whole is not None:
        ins.append(pl.BlockSpec(memory_space=pl.ANY))
        args.append(whole)
        aliases = {3: 0}
    return call(
        place_body,
        (rows // tile,),
        ins,
        pl.BlockSpec((tile, 2 * half), lambda i, s: (i, k)),
        jax.ShapeDtypeStruct((rows, columns), bf16),
        rows * half,
        8 * rows * half,
        aliases,
        name="place",
    )(scalars, *args)


def flip(x, axis):
    return lax.ppermute(x, axis, [(0, 1), (1, 0)])


def flip_x(x, e):
    return lax.ppermute(x, X4, [(i, i ^ e) for i in range(4)])


def per_device(system, row_outer, row_inner, col_outer, col_inner, diag_inverse):
    rows, cols = system.shape
    panel = diag_inverse.shape[0]
    half = panel
    width = half // 4
    chunks = cols // (2 * half)
    xh, xl = lax.axis_index("xh"), lax.axis_index("xl")
    zh, zl = lax.axis_index("zh"), lax.axis_index("zl")
    yh = lax.axis_index("yh")
    y, core = lax.axis_index(Y4), lax.axis_index("core")
    x = 2 * xh + xl
    order = [x ^ e for e in range(4)]
    scalars = [
        jnp.stack(order + [(2 * k + zh) * 4 + o for o in order] + [zh, x]).astype(jnp.int32) for k in range(chunks)
    ]

    def half_of(k, which):
        return lax.dynamic_slice(system, (0, (2 * k + which) * half), (rows, half))

    other = [flip(half_of(k, 1 - zh), "zh") for k in range(chunks)]

    sign_x = (1 - 2 * xh).astype(f32)
    sign_l = (1 - 2 * xl).astype(f32)
    sign_z = (1 - 2 * zh).astype(f32)
    sign_y = (1 - 2 * yh).astype(f32)
    wr = lax.all_gather(jnp.stack([row_outer, row_inner]), ("xh", "zh")).reshape(2, 2, 2, rows) * root_half
    outer, inn = wr[:, :, 0], wr[:, :, 1]
    outer = jnp.where(zh == 0, outer, outer[:, ::-1])
    wrow = jnp.stack(
        [outer[0, 0], outer[0, 1], outer[1, 0] * sign_x, outer[1, 1] * sign_x]
        + [inn[0, 0], inn[0, 1] * sign_z, inn[1, 0], inn[1, 1] * sign_z],
        axis=1,
    )
    wc = lax.all_gather(jnp.stack([col_outer, col_inner]), "xl").reshape(2, 2, chunks, 2, 4, width) * root_half
    wc = lax.dynamic_index_in_dim(wc, zh, 3, keepdims=False)
    wc = lax.dynamic_index_in_dim(wc, x, 3, keepdims=False)
    ones = jnp.ones((width,), f32)
    wcol = [
        jnp.stack(
            [wc[0, 0, k], wc[1, 0, k] * sign_l, wc[0, 1, k], wc[1, 1, k], ones * sign_y, ones, ones, ones]
        )
        for k in range(chunks)
    ]

    left = None
    whole = None
    for k in range(chunks):
        s = scalars[k]
        pieces = split_slices(s, system, other[k], width)
        received = [flip_x(p, e + 1) for e, p in enumerate(pieces)]
        mixed = mix(s, system, other[k], received, wrow, wcol[k])
        full = inner(s, mixed, flip(mixed, "yh"), wcol[k])
        own = full[0:2, 0, :panel]
        hop1 = lax.ppermute(own, "zl", [(0, 1)])
        hop2 = lax.ppermute(hop1, "zl", [(1, 2)])
        hop3 = lax.ppermute(hop2, "zl", [(2, 3)])
        top = jnp.where(zl == 0, own, hop1 + hop2 + hop3)
        if k == 0:
            lead = full[0::2]
            lead = jnp.where(zh == 0, lead, lax.ppermute(lead, "zh", [(0, 1)]))
            up = lax.ppermute(lead, Y4, [(0, 1)])
            down = lax.ppermute(lead, Y4, [(0, 3)])
            far = lax.ppermute(up, Y4, [(1, 2)])
            lead = jnp.where(y == 0, lead, up + down + far)
            lead = jnp.where(core == 0, lead, lax.ppermute(lead, "core", [(0, 1)]))
            left = factor(s, [lead] + [flip_x(lead, e) for e in (1, 2, 3)], diag_inverse)
        done = update(s, full, left, top)
        back = [done[0]] + [flip_x(done[e], e) for e in (1, 2, 3)]
        keep, send = gather_slices(s, back)
        whole = place(s, keep, flip(send, "zh"), whole, k, cols)
    return whole


def solution(mesh):
    fine = Mesh(
        mesh.devices.reshape(2, 2, 4, 2, 2, 2, 2), ("xh", "zh", "zl", "xl", "yh", "yl", "core")
    )
    prow, pcol = ("xh", "zh", "zl"), ("xl", "yh", "yl", "core")
    in_specs = (P(prow, pcol), P(prow), P(prow), P(pcol), P(pcol), P())
    return jax.shard_map(
        per_device, mesh=fine, in_specs=in_specs, out_specs=P(prow, pcol), check_vma=False
    )
```

time: 932 us -> 601 us (0.64)
  waiting for transfers between devices: 850 us -> 300 us
  starting transfers between devices: 13 us -> 121 us
  Pallas kernels: 0 us -> 81.5 us
  blocking collectives: 0 us -> 49.9 us
  local copies, waits for them, and re-layouts: 2.71 us -> 37.3 us
  other arithmetic: 37.8 us -> 8.16 us
  between operations: 14.9 us -> 0.85 us
  matrix products: 13 us -> 0 us
    ppermute x4 -> x56, waiting for transfers between devices: 675 us -> 300 us  [the longest x12 152 us: flip(): return lax.ppermute(x, axis, [(0, 1), (1, 0)])]
    psum x1 -> x0, waiting for transfers between devices: 175 us -> none  [per_device(): top_rows = lax.psum(term.astype(jnp.bfloat16), 'prow')]
    ppermute x4 -> x56, starting transfers between devices: 12.9 us -> 121 us  [the longest x12 37.8 us: flip(): return lax.ppermute(x, axis, [(0, 1), (1, 0)])]
    pallas_call x0 -> x25, Pallas kernels: none -> 81.5 us  [the longest x4 27.5 us: mix(): call(functools.partial(mix_body, sub_rows(tile)), (rows // tile,), ins, o...]
    all_gather x0 -> x2, blocking collectives: none -> 49.9 us  [the longest x1 45.4 us: per_device(): lax.all_gather(jnp.stack([row_outer, row_inner]), ('xh', 'zh'))]
    convert_element_type x5 -> x0, other arithmetic: 37.8 us -> none  [the longest x4 35 us: combine(): return (weights * summed * root_half).astype(jnp.bfloat16)]
    unnamed x10 -> x82, local copies, waits for them, and re-layouts: 2.71 us -> 25.9 us
    dot_general x2 -> x0, matrix products: 13 us -> none  [the longest x1 10.4 us: per_device(): update = jnp.dot(left, top_rows, preferred_element_type=jnp.float32)]
  transfers between devices with their start and end apart: 6 -> 56, of which waited for: 5 -> 23; matrix products, arithmetic and copies ran while one was open for 0% -> 3% of each run, Pallas kernels for 0% -> 12%
where the time goes in v1:
time: 601 us; the launch traced here: 599 us
  waiting for transfers between devices  300 us (50%)
  starting transfers between devices  121 us (20%)
  Pallas kernels  81.5 us (14%)
  blocking collectives  49.9 us (8%)
  local copies, waits for them, and re-layouts  37.3 us (6%)
  other arithmetic  8.16 us (1%)
    ppermute x12, waiting for transfers between devices, flip(): return lax.ppermute(x, axis, [(0, 1), (1, 0)])  152 us
    ppermute x27, waiting for transfers between devices, flip_x(): return lax.ppermute(x, X4, [(i, i ^ e) for i in range(4)])  77.4 us
    ppermute x1, waiting for transfers between devices, per_device(): down = lax.ppermute(lead, Y4, [(0, 3)])  53.4 us
    all_gather x1, blocking collectives, per_device(): lax.all_gather(jnp.stack([row_outer, row_inner]), ('xh', 'zh'))  45.4 us
    ppermute x12, starting transfers between devices, flip(): return lax.ppermute(x, axis, [(0, 1), (1, 0)])  37.8 us
    ppermute x4, starting transfers between devices, per_device(): hop1 = lax.ppermute(own, 'zl', [(0, 1)])  34.5 us
    ppermute x27, starting transfers between devices, flip_x(): return lax.ppermute(x, X4, [(i, i ^ e) for i in range(4)])  33 us
    pallas_call x4, Pallas kernels, mix(): call(functools.partial(mix_body, sub_rows(tile)), (rows // tile,), ins, o...  27.5 us
  transfers between devices with their start and end apart: 56, of which 23 were waited for; matrix products, arithmetic and copies ran while one was open for 3% of the time, Pallas kernels for 12%

profile of v1, /device:TPU:24, one launch (start us, length us, event | category | flops | bytes accessed | tf_op | source)
XLA Modules:
  0.0 599.1 jit_solution(1315653616557294746)
XLA Ops:
  0.0 3.4 constant_dynamic-slice_fusion
  3.4 7.2 %collective-permute-start.5 = (bf16[768,512]{1,0:T(8,128)(2,1)S(1)}, bf16[768,512]{1,0:T(8,128)(2,1)S(1)}, u32[]{:S(2)}, u32[]{:S(2)}) collective-permute-start(bf16[768,512]{1,0:T(8,128)(2,1)S(1)} %get-tuple-element.79), channel_id=1, source_target_pairs={{0,64},{64,0},{1,65},{65,1},{2,66},{66,2},{3,67},{67,3},{4,68},{68... | collective-permute-start | bytes 2359304 | tf_op jit(solution)/shard_map/ppermute | solution.py:249
  10.6 45.4 %all-gather.2 = f32[4,2,768]{2,1,0:T(2,128)S(1)} all-gather(f32[1,2,768]{2,1,0:T(2,128)S(1)} %maximum_bitcast_fusion.1), channel_id=2, replica_groups=mesh['xh'=2,'zh'=2,'zl'=4,'xl'=2,'yh'=2,'yl'=2,'core'=2] {'xh','zh'}, dimensions={0}, use_global_device_ids=true | all-gather | bytes 30720 | tf_op jit(solution)/shard_map/all_gather | solution.py:281
  56.3 4.6 all-gather.3
  61.1 2.8 copy-done
  76.6 5.2 collective-permute-done.7.r2
  84.3 2.8 copy-done.1
  87.0 5.7 mix.5.mine
  94.1 5.8 collective-permute-start.37
  100.1 23.3 %collective-permute-done.9.partner = bf16[4,2,768,128]{3,2,1,0:T(8,128)(2,1)S(1)} collective-permute-done((bf16[4,2,768,128]{3,2,1,0:T(8,128)(2,1)S(1)}, bf16[4,2,768,128]{3,2,1,0:T(8,128)(2,1)S(1)}, u32[]{:S(2)}, u32[]{:S(2)}) %collective-permute-start.9) | collective-permute-done | bytes 1572896 | tf_op jit(solution)/shard_map/ppermute | solution.py:249
  128.5 2.8 copy-done.2
  133.8 3.3 collective-permute-start.39
  139.3 2.8 copy-done.3
  145.3 9.7 %collective-permute-done.39.r2 = bf16[2,768,128]{2,1,0:T(8,128)(2,1)} collective-permute-done((bf16[2,768,128]{2,1,0:T(8,128)(2,1)}, bf16[2,768,128]{2,1,0:T(8,128)(2,1)}, u32[]{:S(2)}, u32[]{:S(2)}) %collective-permute-start.39) | collective-permute-done | bytes 393248 | tf_op jit(solution)/shard_map/ppermute | solution.py:253
  155.0 7.3 %mix.7.mine = bf16[4,2,768,128]{3,2,1,0:T(8,128)(2,1)} custom-call(s32[10]{0:T(128)S(1)} %stack.176.s, bf16[768,4096]{1,0:T(8,128)(2,1)S(1)} %copy-done.3, bf16[768,512]{1,0:T(8,128)(2,1)S(1)} %copy-done.8, bf16[2,768,128]{2,1,0:T(8,128)(2,1)} %collective-permute-done.38.r1, bf16[2,768,128]{2,1,0:T(8,128)(2,1)} %collective-permute-done.39.r2, ...), custom_call_target="tpu_custom_call" | custom-call | flops 6291456 | bytes 3145728 | tf_op jit(solution)/shard_map/mix/pallas_call | solution.py:99
  163.5 13.3 %collective-permute-done.10 = bf16[2,2,768,128]{3,2,1,0:T(8,128)(2,1)} collective-permute-done((bf16[2,2,768,128]{3,2,1,0:T(8,128)(2,1)}, bf16[2,2,768,128]{3,2,1,0:T(8,128)(2,1)}, u32[]{:S(2)}, u32[]{:S(2)}) %collective-permute-start.10) | collective-permute-done | bytes 786464 | tf_op jit(solution)/shard_map/ppermute | solution.py:315
  179.4 25.8 %collective-permute-done.refs_3_.refs_4_.refs_5_.got = bf16[768,512]{1,0:T(8,128)(2,1)S(1)} collective-permute-done((bf16[768,512]{1,0:T(8,128)(2,1)}, bf16[768,512]{1,0:T(8,128)(2,1)S(1)}, u32[]{:S(2)}, u32[]{:S(2)}) %collective-permute-start) | collective-permute-done | bytes 786464 | tf_op jit(solution)/shard_map/ppermute | solution.py:249
  207.2 2.8 copy-done.4
  212.6 2.8 collective-permute-start.2
  218.9 7.3 %mix.6.mine = bf16[4,2,768,128]{3,2,1,0:T(8,128)(2,1)} custom-call(s32[10]{0:T(128)S(1)} %stack.170.s, bf16[768,4096]{1,0:T(8,128)(2,1)S(1)} %copy-done.5, bf16[768,512]{1,0:T(8,128)(2,1)S(1)} %collective-permute-done.25.refs_3_.refs_4_.refs_5_.got, bf16[2,768,128]{2,1,0:T(8,128)(2,1)} %collective-permute-done.26.r1, ...), custom_call_target="tpu_custom_call" | custom-call | flops 6291456 | bytes 3145728 | tf_op jit(solution)/shard_map/mix/pallas_call | solution.py:99
  233.9 3.8 collective-permute-done.3.r3
  238.4 2.8 copy-done.6
  242.8 7.2 %mix.4.mine = bf16[4,2,768,128]{3,2,1,0:T(8,128)(2,1)} custom-call(s32[10]{0:T(128)S(1)} %copy-done.23, bf16[768,4096]{1,0:T(8,128)(2,1)S(1)} %copy-done.6, bf16[768,512]{1,0:T(8,128)(2,1)S(1)} %collective-permute-done.refs_3_.refs_4_.refs_5_.got, bf16[2,768,128]{2,1,0:T(8,128)(2,1)} %collective-permute-done.1.r1, ...), custom_call_target="tpu_custom_call" | custom-call | flops 6291456 | bytes 3145728 | tf_op jit(solution)/shard_map/mix/pallas_call | solution.py:99
  251.8 3.7 inner.7.full
  255.5 53.4 %collective-permute-done.12 = bf16[2,2,768,128]{3,2,1,0:T(8,128)(2,1)} collective-permute-done((bf16[2,2,768,128]{3,2,1,0:T(8,128)(2,1)}, bf16[2,2,768,128]{3,2,1,0:T(8,128)(2,1)}, u32[]{:S(2)}, u32[]{:S(2)}) %collective-permute-start.12) | collective-permute-done | bytes 786464 | tf_op jit(solution)/shard_map/ppermute | solution.py:317
  312.7 30.5 %collective-permute-start.42 = (bf16[2,512,128]{2,1,0:T(8,128)(2,1)S(1)}, bf16[2,512,128]{2,1,0:T(8,128)(2,1)S(1)}, u32[]{:S(2)}, u32[]{:S(2)}) collective-permute-start(bf16[2,512,128]{2,1,0:T(8,128)(2,1)S(1)} %slice_bitcast_fusion.1), channel_id=1, source_target_pairs={{0,16},{1,17},{2,18},{3,19},{4,20},{5,21},{6,22},{7,23},{8,24},{9,... | collective-permute-start | bytes 786440 | tf_op jit(solution)/shard_map/ppermute | solution.py:309
  343.3 3.7 inner.6.full
  352.3 3.4 inner.4.full
  361.5 3.6 collective-permute-done.18
  374.6 21.7 %collective-permute-done.17.p3 = bf16[2,2,768,128]{3,2,1,0:T(8,128)(2,1)} collective-permute-done((bf16[2,2,768,128]{3,2,1,0:T(8,128)(2,1)}, bf16[2,2,768,128]{3,2,1,0:T(8,128)(2,1)}, u32[]{:S(2)}, u32[]{:S(2)}) %collective-permute-start.17) | collective-permute-done | bytes 786464 | tf_op jit(solution)/shard_map/ppermute | solution.py:253
  396.9 6.0 %factor.1.left = bf16[2,2,768,512]{3,2,1,0:T(8,128)(2,1)S(1)} custom-call(s32[10]{0:T(128)S(1)} %stack.164.s, bf16[2,2,768,128]{3,2,1,0:T(8,128)(2,1)} %broadcast_select_fusion.1.p0, bf16[2,2,768,128]{3,2,1,0:T(8,128)(2,1)} %collective-permute-done.15.p1, bf16[2,2,768,128]{3,2,1,0:T(8,128)(2,1)} %collective-permute-done.16.p2, ...), custom_call_target="tpu_custom_call" | custom-call | flops 1610612736 | bytes 6291456 | tf_op jit(solution)/shard_map/factor/pallas_call | solution.py:149
  403.0 3.4 update.7
  406.8 3.2 collective-permute-start.53
  411.3 3.4 update.6
  414.8 3.4 update.5
  421.9 6.5 %collective-permute-done.53.p2 = bf16[2,768,128]{2,1,0:T(8,128)(2,1)S(1)} collective-permute-done((bf16[2,768,128]{2,1,0:T(8,128)(2,1)S(1)}, bf16[2,768,128]{2,1,0:T(8,128)(2,1)S(1)}, u32[]{:S(2)}, u32[]{:S(2)}) %collective-permute-start.53) | collective-permute-done | bytes 393248 | tf_op jit(solution)/shard_map/ppermute | solution.py:253
  431.1 4.3 collective-permute-done.45.p1
  437.5 3.3 update.4
  440.8 3.0 collective-permute-done.33.p1
  444.1 9.7 %collective-permute-done.34.p2 = bf16[2,768,128]{2,1,0:T(8,128)(2,1)S(1)} collective-permute-done((bf16[2,768,128]{2,1,0:T(8,128)(2,1)S(1)}, bf16[2,768,128]{2,1,0:T(8,128)(2,1)S(1)}, u32[]{:S(2)}, u32[]{:S(2)}) %collective-permute-start.34) | collective-permute-done | bytes 393248 | tf_op jit(solution)/shard_map/ppermute | solution.py:253
  458.1 4.1 collective-permute-done.46.p2
  462.2 6.2 %collective-permute-start.36 = (bf16[768,512]{1,0:T(8,128)(2,1)S(1)}, bf16[768,512]{1,0:T(8,128)(2,1)S(1)}, u32[]{:S(2)}, u32[]{:S(2)}) collective-permute-start(bf16[768,512]{1,0:T(8,128)(2,1)S(1)} %get-tuple-element.61), channel_id=1, source_target_pairs={{0,64},{64,0},{1,65},{65,1},{2,66},{66,2},{3,67},{67,3},{4,68},{68... | collective-permute-start | bytes 2359304 | tf_op jit(solution)/shard_map/ppermute | solution.py:249
  468.5 4.5 collective-permute-start.55
  476.5 3.1 collective-permute-done.23.p3
  480.7 6.3 %collective-permute-start.24 = (bf16[768,512]{1,0:T(8,128)(2,1)S(1)}, bf16[768,512]{1,0:T(8,128)(2,1)S(1)}, u32[]{:S(2)}, u32[]{:S(2)}) collective-permute-start(bf16[768,512]{1,0:T(8,128)(2,1)S(1)} %get-tuple-element.52), channel_id=1, source_target_pairs={{0,64},{64,0},{1,65},{65,1},{2,66},{66,2},{3,67},{67,3},{4,68},{68... | collective-permute-start | bytes 2359304 | tf_op jit(solution)/shard_map/ppermute | solution.py:249
  487.0 76.3 %collective-permute-done.55.got = bf16[768,512]{1,0:T(8,128)(2,1)S(1)} collective-permute-done((bf16[768,512]{1,0:T(8,128)(2,1)S(1)}, bf16[768,512]{1,0:T(8,128)(2,1)S(1)}, u32[]{:S(2)}, u32[]{:S(2)}) %collective-permute-start.55) | collective-permute-done | bytes 786464 | tf_op jit(solution)/shard_map/ppermute | solution.py:249
  565.5 14.6 %collective-permute-done.48.got = bf16[768,512]{1,0:T(8,128)(2,1)S(1)} collective-permute-done((bf16[768,512]{1,0:T(8,128)(2,1)S(1)}, bf16[768,512]{1,0:T(8,128)(2,1)S(1)}, u32[]{:S(2)}, u32[]{:S(2)}) %collective-permute-start.48) | collective-permute-done | bytes 786464 | tf_op jit(solution)/shard_map/ppermute | solution.py:249
  584.6 12.2 %collective-permute-done.24.got = bf16[768,512]{1,0:T(8,128)(2,1)S(1)} collective-permute-done((bf16[768,512]{1,0:T(8,128)(2,1)S(1)}, bf16[768,512]{1,0:T(8,128)(2,1)S(1)}, u32[]{:S(2)}, u32[]{:S(2)}) %collective-permute-start.24) | collective-permute-done | bytes 786464 | tf_op jit(solution)/shard_map/ppermute | solution.py:249
  (214 shorter events, 107.0 us)
Async XLA Ops:
  3.4 57.7 %collective-permute-start.5 = (bf16[768,512]{1,0:T(8,128)(2,1)S(1)}, bf16[768,512]{1,0:T(8,128)(2,1)S(1)}, u32[]{:S(2)}, u32[]{:S(2)}) collective-permute-start(bf16[768,512]{1,0:T(8,128)(2,1)S(1)} %get-tuple-element.79), channel_id=1, source_target_pairs={{0,64},{64,0},{1,65},{65,1},{2,66},{66,2},{3,67},{67,3},{4,68},{68... | collective-permute-start | bytes 2359304 | tf_op jit(solution)/shard_map/ppermute | solution.py:249
  65.2 11.3 %collective-permute-start.6 = (bf16[2,768,128]{2,1,0:T(8,128)(2,1)S(1)}, bf16[2,768,128]{2,1,0:T(8,128)(2,1)S(1)}, u32[]{:S(2)}, u32[]{:S(2)}) collective-permute-start(bf16[2,768,128]{2,1,0:T(8,128)(2,1)S(1)} %get-tuple-element.44), channel_id=1, source_target_pairs={{0,8},{8,0},{128,136},{136,128},{1,9},{9,1},{129,137},{137,129},{2... | collective-permute-start | bytes 1179656 | tf_op jit(solution)/shard_map/ppermute | solution.py:253
  66.7 15.0 %collective-permute-start.7 = (bf16[2,768,128]{2,1,0:T(8,128)(2,1)S(1)}, bf16[2,768,128]{2,1,0:T(8,128)(2,1)S(1)}, u32[]{:S(2)}, u32[]{:S(2)}) collective-permute-start(bf16[2,768,128]{2,1,0:T(8,128)(2,1)S(1)} %get-tuple-element.45), channel_id=1, source_target_pairs={{0,128},{8,136},{128,0},{136,8},{1,129},{9,137},{129,1},{137,9},{2... | collective-permute-start | bytes 1179656 | tf_op jit(solution)/shard_map/ppermute | solution.py:253
  69.4 14.8 %collective-permute-start.8 = (bf16[2,768,128]{2,1,0:T(8,128)(2,1)S(1)}, bf16[2,768,128]{2,1,0:T(8,128)(2,1)S(1)}, u32[]{:S(2)}, u32[]{:S(2)}) collective-permute-start(bf16[2,768,128]{2,1,0:T(8,128)(2,1)S(1)} %get-tuple-element.46), channel_id=1, source_target_pairs={{0,136},{8,128},{128,8},{136,0},{1,137},{9,129},{129,9},{137,1},{2... | collective-permute-start | bytes 1179656 | tf_op jit(solution)/shard_map/ppermute | solution.py:253
  92.8 30.6 %collective-permute-start.9 = (bf16[4,2,768,128]{3,2,1,0:T(8,128)(2,1)S(1)}, bf16[4,2,768,128]{3,2,1,0:T(8,128)(2,1)S(1)}, u32[]{:S(2)}, u32[]{:S(2)}) collective-permute-start(bf16[4,2,768,128]{3,2,1,0:T(8,128)(2,1)S(1)} %mix.5.mine), channel_id=1, source_target_pairs={{0,4},{4,0},{1,5},{5,1},{2,6},{6,2},{3,7},{7,3},{8,12},{12,8},{9,1... | collective-permute-start | bytes 4718600 | tf_op jit(solution)/shard_map/ppermute | solution.py:249
  94.1 34.4 %collective-permute-start.37 = (bf16[768,512]{1,0:T(8,128)(2,1)}, bf16[768,512]{1,0:T(8,128)(2,1)S(1)}, u32[]{:S(2)}, u32[]{:S(2)}) collective-permute-start(bf16[768,512]{1,0:T(8,128)(2,1)} %get-tuple-element.77), channel_id=1, source_target_pairs={{0,64},{64,0},{1,65},{65,1},{2,66},{66,2},{3,67},{67,3},{4,68},{68... | collective-permute-start | bytes 2359304 | tf_op jit(solution)/shard_map/ppermute | solution.py:249
  99.9 38.6 %collective-permute-start.25 = (bf16[768,512]{1,0:T(8,128)(2,1)}, bf16[768,512]{1,0:T(8,128)(2,1)S(1)}, u32[]{:S(2)}, u32[]{:S(2)}) collective-permute-start(bf16[768,512]{1,0:T(8,128)(2,1)} %get-tuple-element.78), channel_id=1, source_target_pairs={{0,64},{64,0},{1,65},{65,1},{2,66},{66,2},{3,67},{67,3},{4,68},{68... | collective-permute-start | bytes 2359304 | tf_op jit(solution)/shard_map/ppermute | solution.py:249
  126.2 50.6 %collective-permute-start.10 = (bf16[2,2,768,128]{3,2,1,0:T(8,128)(2,1)}, bf16[2,2,768,128]{3,2,1,0:T(8,128)(2,1)}, u32[]{:S(2)}, u32[]{:S(2)}) collective-permute-start(bf16[2,2,768,128]{3,2,1,0:T(8,128)(2,1)} %slice.111), channel_id=1, source_target_pairs={{0,64},{1,65},{2,66},{3,67},{4,68},{5,69},{6,70},{7,71},{8,72},{9,... | collective-permute-start | bytes 2359304 | tf_op jit(solution)/shard_map/ppermute | solution.py:315
  133.8 11.5 %collective-permute-start.38 = (bf16[2,768,128]{2,1,0:T(8,128)(2,1)}, bf16[2,768,128]{2,1,0:T(8,128)(2,1)}, u32[]{:S(2)}, u32[]{:S(2)}) collective-permute-start(bf16[2,768,128]{2,1,0:T(8,128)(2,1)} %get-tuple-element.62), channel_id=1, source_target_pairs={{0,8},{8,0},{128,136},{136,128},{1,9},{9,1},{129,137},{137,129},{2... | collective-permute-start | bytes 1179656 | tf_op jit(solution)/shard_map/ppermute | solution.py:253
  133.8 21.2 %collective-permute-start.39 = (bf16[2,768,128]{2,1,0:T(8,128)(2,1)}, bf16[2,768,128]{2,1,0:T(8,128)(2,1)}, u32[]{:S(2)}, u32[]{:S(2)}) collective-permute-start(bf16[2,768,128]{2,1,0:T(8,128)(2,1)} %get-tuple-element.63), channel_id=1, source_target_pairs={{0,128},{8,136},{128,0},{136,8},{1,129},{9,137},{129,1},{137,9},{2... | collective-permute-start | bytes 1179656 | tf_op jit(solution)/shard_map/ppermute | solution.py:253
  137.1 17.9 %collective-permute-start.40 = (bf16[2,768,128]{2,1,0:T(8,128)(2,1)}, bf16[2,768,128]{2,1,0:T(8,128)(2,1)}, u32[]{:S(2)}, u32[]{:S(2)}) collective-permute-start(bf16[2,768,128]{2,1,0:T(8,128)(2,1)} %get-tuple-element.64), channel_id=1, source_target_pairs={{0,136},{8,128},{128,8},{136,0},{1,137},{9,129},{129,9},{137,1},{2... | collective-permute-start | bytes 1179656 | tf_op jit(solution)/shard_map/ppermute | solution.py:253
  138.5 66.8 %collective-permute-start = (bf16[768,512]{1,0:T(8,128)(2,1)}, bf16[768,512]{1,0:T(8,128)(2,1)S(1)}, u32[]{:S(2)}, u32[]{:S(2)}) collective-permute-start(bf16[768,512]{1,0:T(8,128)(2,1)} %get-tuple-element.80), channel_id=1, source_target_pairs={{0,64},{64,0},{1,65},{65,1},{2,66},{66,2},{3,67},{67,3},{4,68},{68... | collective-permute-start | bytes 2359304 | tf_op jit(solution)/shard_map/ppermute | solution.py:249
  145.3 67.2 %collective-permute-start.26 = (bf16[2,768,128]{2,1,0:T(8,128)(2,1)}, bf16[2,768,128]{2,1,0:T(8,128)(2,1)}, u32[]{:S(2)}, u32[]{:S(2)}) collective-permute-start(bf16[2,768,128]{2,1,0:T(8,128)(2,1)} %get-tuple-element.53), channel_id=1, source_target_pairs={{0,8},{8,0},{128,136},{136,128},{1,9},{9,1},{129,137},{137,129},{2... | collective-permute-start | bytes 1179656 | tf_op jit(solution)/shard_map/ppermute | solution.py:253
  155.0 57.6 %collective-permute-start.27 = (bf16[2,768,128]{2,1,0:T(8,128)(2,1)}, bf16[2,768,128]{2,1,0:T(8,128)(2,1)}, u32[]{:S(2)}, u32[]{:S(2)}) collective-permute-start(bf16[2,768,128]{2,1,0:T(8,128)(2,1)} %get-tuple-element.54), channel_id=1, source_target_pairs={{0,128},{8,136},{128,0},{136,8},{1,129},{9,137},{129,1},{137,9},{2... | collective-permute-start | bytes 1179656 | tf_op jit(solution)/shard_map/ppermute | solution.py:253
  162.3 89.0 %collective-permute-start.41 = (bf16[4,2,768,128]{3,2,1,0:T(8,128)(2,1)}, bf16[4,2,768,128]{3,2,1,0:T(8,128)(2,1)}, u32[]{:S(2)}, u32[]{:S(2)}) collective-permute-start(bf16[4,2,768,128]{3,2,1,0:T(8,128)(2,1)} %mix.7.mine), channel_id=1, source_target_pairs={{0,4},{4,0},{1,5},{5,1},{2,6},{6,2},{3,7},{7,3},{8,12},{12,8},{9,1... | collective-permute-start | bytes 4718600 | tf_op jit(solution)/shard_map/ppermute | solution.py:249
  177.9 53.8 %collective-permute-start.11 = (bf16[2,2,768,128]{3,2,1,0:T(8,128)(2,1)}, bf16[2,2,768,128]{3,2,1,0:T(8,128)(2,1)}, u32[]{:S(2)}, u32[]{:S(2)}) collective-permute-start(bf16[2,2,768,128]{3,2,1,0:T(8,128)(2,1)} %broadcast_select_fusion), channel_id=1, source_target_pairs={{0,2},{1,3},{8,10},{9,11},{16,18},{17,19},{24,26},{25,27},{32,34},... | collective-permute-start | bytes 2359304 | tf_op jit(solution)/shard_map/ppermute | solution.py:316
  205.3 10.8 %collective-permute-start.28 = (bf16[2,768,128]{2,1,0:T(8,128)(2,1)}, bf16[2,768,128]{2,1,0:T(8,128)(2,1)}, u32[]{:S(2)}, u32[]{:S(2)}) collective-permute-start(bf16[2,768,128]{2,1,0:T(8,128)(2,1)} %get-tuple-element.55), channel_id=1, source_target_pairs={{0,136},{8,128},{128,8},{136,0},{1,137},{9,129},{129,9},{137,1},{2... | collective-permute-start | bytes 1179656 | tf_op jit(solution)/shard_map/ppermute | solution.py:253
  212.5 16.0 %collective-permute-start.1 = (bf16[2,768,128]{2,1,0:T(8,128)(2,1)}, bf16[2,768,128]{2,1,0:T(8,128)(2,1)}, u32[]{:S(2)}, u32[]{:S(2)}) collective-permute-start(bf16[2,768,128]{2,1,0:T(8,128)(2,1)} %get-tuple-element.41), channel_id=1, source_target_pairs={{0,8},{8,0},{128,136},{136,128},{1,9},{9,1},{129,137},{137,129},{2... | collective-permute-start | bytes 1179656 | tf_op jit(solution)/shard_map/ppermute | solution.py:253
  212.6 17.8 %collective-permute-start.2 = (bf16[2,768,128]{2,1,0:T(8,128)(2,1)}, bf16[2,768,128]{2,1,0:T(8,128)(2,1)}, u32[]{:S(2)}, u32[]{:S(2)}) collective-permute-start(bf16[2,768,128]{2,1,0:T(8,128)(2,1)} %get-tuple-element.42), channel_id=1, source_target_pairs={{0,128},{8,136},{128,0},{136,8},{1,129},{9,137},{129,1},{137,9},{2... | collective-permute-start | bytes 1179656 | tf_op jit(solution)/shard_map/ppermute | solution.py:253
  226.2 117.1 %collective-permute-start.29 = (bf16[4,2,768,128]{3,2,1,0:T(8,128)(2,1)}, bf16[4,2,768,128]{3,2,1,0:T(8,128)(2,1)}, u32[]{:S(2)}, u32[]{:S(2)}) collective-permute-start(bf16[4,2,768,128]{3,2,1,0:T(8,128)(2,1)} %mix.6.mine), channel_id=1, source_target_pairs={{0,4},{4,0},{1,5},{5,1},{2,6},{6,2},{3,7},{7,3},{8,12},{12,8},{9,1... | collective-permute-start | bytes 4718600 | tf_op jit(solution)/shard_map/ppermute | solution.py:249
  230.4 78.5 %collective-permute-start.12 = (bf16[2,2,768,128]{3,2,1,0:T(8,128)(2,1)}, bf16[2,2,768,128]{3,2,1,0:T(8,128)(2,1)}, u32[]{:S(2)}, u32[]{:S(2)}) collective-permute-start(bf16[2,2,768,128]{3,2,1,0:T(8,128)(2,1)} %broadcast_select_fusion), channel_id=1, source_target_pairs={{0,6},{1,7},{8,14},{9,15},{16,22},{17,23},{24,30},{25,31},{32,38},... | collective-permute-start | bytes 2359304 | tf_op jit(solution)/shard_map/ppermute | solution.py:317
  231.7 77.2 %collective-permute-start.13 = (bf16[2,2,768,128]{3,2,1,0:T(8,128)(2,1)}, bf16[2,2,768,128]{3,2,1,0:T(8,128)(2,1)}, u32[]{:S(2)}, u32[]{:S(2)}) collective-permute-start(bf16[2,2,768,128]{3,2,1,0:T(8,128)(2,1)} %collective-permute-done.11), channel_id=1, source_target_pairs={{2,4},{3,5},{10,12},{11,13},{18,20},{19,21},{26,28},{27,29},{34,36... | collective-permute-start | bytes 2359304 | tf_op jit(solution)/shard_map/ppermute | solution.py:318
  250.0 99.6 %collective-permute-start.4 = (bf16[4,2,768,128]{3,2,1,0:T(8,128)(2,1)}, bf16[4,2,768,128]{3,2,1,0:T(8,128)(2,1)S(1)}, u32[]{:S(2)}, u32[]{:S(2)}) collective-permute-start(bf16[4,2,768,128]{3,2,1,0:T(8,128)(2,1)} %mix.4.mine), channel_id=1, source_target_pairs={{0,4},{4,0},{1,5},{5,1},{2,6},{6,2},{3,7},{7,3},{8,12},{12,8},{9,1... | collective-permute-start | bytes 4718600 | tf_op jit(solution)/shard_map/ppermute | solution.py:249
  310.7 47.8 %collective-permute-start.14 = (bf16[2,2,768,128]{3,2,1,0:T(8,128)(2,1)S(1)}, bf16[2,2,768,128]{3,2,1,0:T(8,128)(2,1)S(1)}, u32[]{:S(2)}, u32[]{:S(2)}) collective-permute-start(bf16[2,2,768,128]{3,2,1,0:T(8,128)(2,1)S(1)} %add_select_fusion), channel_id=1, source_target_pairs={{0,1},{2,3},{4,5},{6,7},{8,9},{10,11},{12,13},{14,15},{16,17},{18,... | collective-permute-start | bytes 2359304 | tf_op jit(solution)/shard_map/ppermute | solution.py:320
  312.7 44.3 %collective-permute-start.42 = (bf16[2,512,128]{2,1,0:T(8,128)(2,1)S(1)}, bf16[2,512,128]{2,1,0:T(8,128)(2,1)S(1)}, u32[]{:S(2)}, u32[]{:S(2)}) collective-permute-start(bf16[2,512,128]{2,1,0:T(8,128)(2,1)S(1)} %slice_bitcast_fusion.1), channel_id=1, source_target_pairs={{0,16},{1,17},{2,18},{3,19},{4,20},{5,21},{6,22},{7,23},{8,24},{9,... | collective-permute-start | bytes 786440 | tf_op jit(solution)/shard_map/ppermute | solution.py:309
  347.0 10.8 %collective-permute-start.30 = (bf16[2,512,128]{2,1,0:T(8,128)(2,1)S(1)}, bf16[2,512,128]{2,1,0:T(8,128)(2,1)S(1)}, u32[]{:S(2)}, u32[]{:S(2)}) collective-permute-start(bf16[2,512,128]{2,1,0:T(8,128)(2,1)S(1)} %slice_bitcast_fusion.2), channel_id=1, source_target_pairs={{0,16},{1,17},{2,18},{3,19},{4,20},{5,21},{6,22},{7,23},{8,24},{9,... | collective-permute-start | bytes 786440 | tf_op jit(solution)/shard_map/ppermute | solution.py:309
  348.3 13.2 %collective-permute-start.49 = (bf16[2,512,128]{2,1,0:T(8,128)(2,1)S(1)}, bf16[2,512,128]{2,1,0:T(8,128)(2,1)S(1)}, u32[]{:S(2)}, u32[]{:S(2)}) collective-permute-start(bf16[2,512,128]{2,1,0:T(8,128)(2,1)S(1)} %slice_bitcast_fusion), channel_id=1, source_target_pairs={{0,16},{1,17},{2,18},{3,19},{4,20},{5,21},{6,22},{7,23},{8,24},{9,... | collective-permute-start | bytes 786440 | tf_op jit(solution)/shard_map/ppermute | solution.py:309
  359.4 36.9 %collective-permute-start.17 = (bf16[2,2,768,128]{3,2,1,0:T(8,128)(2,1)}, bf16[2,2,768,128]{3,2,1,0:T(8,128)(2,1)}, u32[]{:S(2)}, u32[]{:S(2)}) collective-permute-start(bf16[2,2,768,128]{3,2,1,0:T(8,128)(2,1)} %broadcast_select_fusion.1.p0), channel_id=1, source_target_pairs={{0,136},{8,128},{128,8},{136,0},{1,137},{9,129},{129,9},{137,1},{2... | collective-permute-start | bytes 2359304 | tf_op jit(solution)/shard_map/ppermute | solution.py:253
  361.5 34.8 %collective-permute-start.16 = (bf16[2,2,768,128]{3,2,1,0:T(8,128)(2,1)}, bf16[2,2,768,128]{3,2,1,0:T(8,128)(2,1)}, u32[]{:S(2)}, u32[]{:S(2)}) collective-permute-start(bf16[2,2,768,128]{3,2,1,0:T(8,128)(2,1)} %broadcast_select_fusion.1.p0), channel_id=1, source_target_pairs={{0,128},{8,136},{128,0},{136,8},{1,129},{9,137},{129,1},{137,9},{2... | collective-permute-start | bytes 2359304 | tf_op jit(solution)/shard_map/ppermute | solution.py:253
  365.1 31.8 %collective-permute-start.15 = (bf16[2,2,768,128]{3,2,1,0:T(8,128)(2,1)}, bf16[2,2,768,128]{3,2,1,0:T(8,128)(2,1)}, u32[]{:S(2)}, u32[]{:S(2)}) collective-permute-start(bf16[2,2,768,128]{3,2,1,0:T(8,128)(2,1)} %broadcast_select_fusion.1.p0), channel_id=1, source_target_pairs={{0,8},{8,0},{128,136},{136,128},{1,9},{9,1},{129,137},{137,129},{2... | collective-permute-start | bytes 2359304 | tf_op jit(solution)/shard_map/ppermute | solution.py:253
  372.0 38.0 %collective-permute-start.32 = (bf16[2,512,128]{2,1,0:T(8,128)(2,1)}, bf16[2,512,128]{2,1,0:T(8,128)(2,1)S(1)}, u32[]{:S(2)}, u32[]{:S(2)}) collective-permute-start(bf16[2,512,128]{2,1,0:T(8,128)(2,1)} %copy-done.29), channel_id=1, source_target_pairs={{32,48},{33,49},{34,50},{35,51},{36,52},{37,53},{38,54},{39,55},{4... | collective-permute-start | bytes 786440 | tf_op jit(solution)/shard_map/ppermute | solution.py:311
  372.7 45.5 %collective-permute-start.20 = (bf16[2,512,128]{2,1,0:T(8,128)(2,1)}, bf16[2,512,128]{2,1,0:T(8,128)(2,1)S(1)}, u32[]{:S(2)}, u32[]{:S(2)}) collective-permute-start(bf16[2,512,128]{2,1,0:T(8,128)(2,1)} %collective-permute-done.19), channel_id=1, source_target_pairs={{32,48},{33,49},{34,50},{35,51},{36,52},{37,53},{38,54},{39,55},{4... | collective-permute-start | bytes 786440 | tf_op jit(solution)/shard_map/ppermute | solution.py:311
  406.4 13.9 %collective-permute-start.52 = (bf16[2,768,128]{2,1,0:T(8,128)(2,1)S(1)}, bf16[2,768,128]{2,1,0:T(8,128)(2,1)S(1)}, u32[]{:S(2)}, u32[]{:S(2)}) collective-permute-start(bf16[2,768,128]{2,1,0:T(8,128)(2,1)S(1)} %get-tuple-element.72), channel_id=1, source_target_pairs={{0,8},{8,0},{128,136},{136,128},{1,9},{9,1},{129,137},{137,129},{2... | collective-permute-start | bytes 1179656 | tf_op jit(solution)/shard_map/ppermute | solution.py:253
  406.8 21.6 %collective-permute-start.53 = (bf16[2,768,128]{2,1,0:T(8,128)(2,1)S(1)}, bf16[2,768,128]{2,1,0:T(8,128)(2,1)S(1)}, u32[]{:S(2)}, u32[]{:S(2)}) collective-permute-start(bf16[2,768,128]{2,1,0:T(8,128)(2,1)S(1)} %get-tuple-element.73), channel_id=1, source_target_pairs={{0,128},{8,136},{128,0},{136,8},{1,129},{9,137},{129,1},{137,9},{2... | collective-permute-start | bytes 1179656 | tf_op jit(solution)/shard_map/ppermute | solution.py:253
  410.1 20.5 %collective-permute-start.54 = (bf16[2,768,128]{2,1,0:T(8,128)(2,1)S(1)}, bf16[2,768,128]{2,1,0:T(8,128)(2,1)S(1)}, u32[]{:S(2)}, u32[]{:S(2)}) collective-permute-start(bf16[2,768,128]{2,1,0:T(8,128)(2,1)S(1)} %get-tuple-element.74), channel_id=1, source_target_pairs={{0,136},{8,128},{128,8},{136,0},{1,137},{9,129},{129,9},{137,1},{2... | collective-permute-start | bytes 1179656 | tf_op jit(solution)/shard_map/ppermute | solution.py:253
  414.7 20.6 %collective-permute-start.45 = (bf16[2,768,128]{2,1,0:T(8,128)(2,1)S(1)}, bf16[2,768,128]{2,1,0:T(8,128)(2,1)S(1)}, u32[]{:S(2)}, u32[]{:S(2)}) collective-permute-start(bf16[2,768,128]{2,1,0:T(8,128)(2,1)S(1)} %get-tuple-element.66), channel_id=1, source_target_pairs={{0,8},{8,0},{128,136},{136,128},{1,9},{9,1},{129,137},{137,129},{2... | collective-permute-start | bytes 1179656 | tf_op jit(solution)/shard_map/ppermute | solution.py:253
  418.2 25.6 %collective-permute-start.33 = (bf16[2,768,128]{2,1,0:T(8,128)(2,1)S(1)}, bf16[2,768,128]{2,1,0:T(8,128)(2,1)S(1)}, u32[]{:S(2)}, u32[]{:S(2)}) collective-permute-start(bf16[2,768,128]{2,1,0:T(8,128)(2,1)S(1)} %get-tuple-element.57), channel_id=1, source_target_pairs={{0,8},{8,0},{128,136},{136,128},{1,9},{9,1},{129,137},{137,129},{2... | collective-permute-start | bytes 1179656 | tf_op jit(solution)/shard_map/ppermute | solution.py:253
  420.3 33.6 %collective-permute-start.34 = (bf16[2,768,128]{2,1,0:T(8,128)(2,1)S(1)}, bf16[2,768,128]{2,1,0:T(8,128)(2,1)S(1)}, u32[]{:S(2)}, u32[]{:S(2)}) collective-permute-start(bf16[2,768,128]{2,1,0:T(8,128)(2,1)S(1)} %get-tuple-element.58), channel_id=1, source_target_pairs={{0,128},{8,136},{128,0},{136,8},{1,129},{9,137},{129,1},{137,9},{2... | collective-permute-start | bytes 1179656 | tf_op jit(solution)/shard_map/ppermute | solution.py:253
  428.5 25.7 %collective-permute-start.35 = (bf16[2,768,128]{2,1,0:T(8,128)(2,1)S(1)}, bf16[2,768,128]{2,1,0:T(8,128)(2,1)S(1)}, u32[]{:S(2)}, u32[]{:S(2)}) collective-permute-start(bf16[2,768,128]{2,1,0:T(8,128)(2,1)S(1)} %get-tuple-element.59), channel_id=1, source_target_pairs={{0,136},{8,128},{128,8},{136,0},{1,137},{9,129},{129,9},{137,1},{2... | collective-permute-start | bytes 1179656 | tf_op jit(solution)/shard_map/ppermute | solution.py:253
  430.7 31.6 %collective-permute-start.46 = (bf16[2,768,128]{2,1,0:T(8,128)(2,1)S(1)}, bf16[2,768,128]{2,1,0:T(8,128)(2,1)S(1)}, u32[]{:S(2)}, u32[]{:S(2)}) collective-permute-start(bf16[2,768,128]{2,1,0:T(8,128)(2,1)S(1)} %get-tuple-element.67), channel_id=1, source_target_pairs={{0,128},{8,136},{128,0},{136,8},{1,129},{9,137},{129,1},{137,9},{2... | collective-permute-start | bytes 1179656 | tf_op jit(solution)/shard_map/ppermute | solution.py:253
  435.4 33.1 %collective-permute-start.47 = (bf16[2,768,128]{2,1,0:T(8,128)(2,1)S(1)}, bf16[2,768,128]{2,1,0:T(8,128)(2,1)S(1)}, u32[]{:S(2)}, u32[]{:S(2)}) collective-permute-start(bf16[2,768,128]{2,1,0:T(8,128)(2,1)S(1)} %get-tuple-element.68), channel_id=1, source_target_pairs={{0,136},{8,128},{128,8},{136,0},{1,137},{9,129},{129,9},{137,1},{2... | collective-permute-start | bytes 1179656 | tf_op jit(solution)/shard_map/ppermute | solution.py:253
  443.8 30.2 %collective-permute-start.21 = (bf16[2,768,128]{2,1,0:T(8,128)(2,1)S(1)}, bf16[2,768,128]{2,1,0:T(8,128)(2,1)S(1)}, u32[]{:S(2)}, u32[]{:S(2)}) collective-permute-start(bf16[2,768,128]{2,1,0:T(8,128)(2,1)S(1)} %get-tuple-element.48), channel_id=1, source_target_pairs={{0,8},{8,0},{128,136},{136,128},{1,9},{9,1},{129,137},{137,129},{2... | collective-permute-start | bytes 1179656 | tf_op jit(solution)/shard_map/ppermute | solution.py:253
  453.9 22.6 %collective-permute-start.22 = (bf16[2,768,128]{2,1,0:T(8,128)(2,1)S(1)}, bf16[2,768,128]{2,1,0:T(8,128)(2,1)S(1)}, u32[]{:S(2)}, u32[]{:S(2)}) collective-permute-start(bf16[2,768,128]{2,1,0:T(8,128)(2,1)S(1)} %get-tuple-element.49), channel_id=1, source_target_pairs={{0,128},{8,136},{128,0},{136,8},{1,129},{9,137},{129,1},{137,9},{2... | collective-permute-start | bytes 1179656 | tf_op jit(solution)/shard_map/ppermute | solution.py:253
  454.2 25.4 %collective-permute-start.23 = (bf16[2,768,128]{2,1,0:T(8,128)(2,1)S(1)}, bf16[2,768,128]{2,1,0:T(8,128)(2,1)S(1)}, u32[]{:S(2)}, u32[]{:S(2)}) collective-permute-start(bf16[2,768,128]{2,1,0:T(8,128)(2,1)S(1)} %get-tuple-element.50), channel_id=1, source_target_pairs={{0,136},{8,128},{128,8},{136,0},{1,137},{9,129},{129,9},{137,1},{2... | collective-permute-start | bytes 1179656 | tf_op jit(solution)/shard_map/ppermute | solution.py:253
  462.2 120.2 %collective-permute-start.36 = (bf16[768,512]{1,0:T(8,128)(2,1)S(1)}, bf16[768,512]{1,0:T(8,128)(2,1)S(1)}, u32[]{:S(2)}, u32[]{:S(2)}) collective-permute-start(bf16[768,512]{1,0:T(8,128)(2,1)S(1)} %get-tuple-element.61), channel_id=1, source_target_pairs={{0,64},{64,0},{1,65},{65,1},{2,66},{66,2},{3,67},{67,3},{4,68},{68... | collective-permute-start | bytes 2359304 | tf_op jit(solution)/shard_map/ppermute | solution.py:249
  468.5 94.8 %collective-permute-start.55 = (bf16[768,512]{1,0:T(8,128)(2,1)S(1)}, bf16[768,512]{1,0:T(8,128)(2,1)S(1)}, u32[]{:S(2)}, u32[]{:S(2)}) collective-permute-start(bf16[768,512]{1,0:T(8,128)(2,1)S(1)} %get-tuple-element.76), channel_id=1, source_target_pairs={{0,64},{64,0},{1,65},{65,1},{2,66},{66,2},{3,67},{67,3},{4,68},{68... | collective-permute-start | bytes 2359304 | tf_op jit(solution)/shard_map/ppermute | solution.py:249
  474.0 106.1 %collective-permute-start.48 = (bf16[768,512]{1,0:T(8,128)(2,1)S(1)}, bf16[768,512]{1,0:T(8,128)(2,1)S(1)}, u32[]{:S(2)}, u32[]{:S(2)}) collective-permute-start(bf16[768,512]{1,0:T(8,128)(2,1)S(1)} %get-tuple-element.70), channel_id=1, source_target_pairs={{0,64},{64,0},{1,65},{65,1},{2,66},{66,2},{3,67},{67,3},{4,68},{68... | collective-permute-start | bytes 2359304 | tf_op jit(solution)/shard_map/ppermute | solution.py:249
  480.7 116.2 %collective-permute-start.24 = (bf16[768,512]{1,0:T(8,128)(2,1)S(1)}, bf16[768,512]{1,0:T(8,128)(2,1)S(1)}, u32[]{:S(2)}, u32[]{:S(2)}) collective-permute-start(bf16[768,512]{1,0:T(8,128)(2,1)S(1)} %get-tuple-element.52), channel_id=1, source_target_pairs={{0,64},{64,0},{1,65},{65,1},{2,66},{66,2},{3,67},{67,3},{4,68},{68... | collective-permute-start | bytes 2359304 | tf_op jit(solution)/shard_map/ppermute | solution.py:249
  (49 other events, 693.4 us)

commit v2 on v0

v2 whole, which is shorter than its diff:
```python
import functools
import jax
import jax.numpy as jnp
from jax import lax
from jax.experimental import pallas as pl
from jax.experimental.pallas import tpu as pltpu
from jax.sharding import Mesh, PartitionSpec as P

root_half = 0.7071067811865476
f32, bf16 = jnp.float32, jnp.bfloat16
X4 = ("xh", "xl")
COLS = ("xl", "yh", "yl", "core")


def rows_of(total):
    for tile in (192, 96, 64, 48, 32, 16, 8):
        if total % tile == 0:
            return tile
    return total


def small_rows_of(total):
    tile = rows_of(total)
    return tile // 2 if tile % 32 == 0 else tile


def sub_rows(tile):
    return 16 if tile % 16 == 0 else 8


def call(body, grid, ins, outs, shapes, flops, nbytes, aliases=None):
    return pl.pallas_call(
        body,
        grid=grid,
        in_specs=ins,
        out_specs=outs,
        out_shape=shapes,
        input_output_aliases=aliases or {},
        cost_estimate=pl.CostEstimate(flops=flops, bytes_accessed=nbytes, transcendentals=0),
        compiler_params=pltpu.CompilerParams(vmem_limit_bytes=8 * 1024 * 1024),
    )


def split_body(z, mine, other, out):
    zh = z[0]
    width = out.shape[3]
    for j in range(4):
        at = slice(j * width, (j + 1) * width)
        out[j, zh] = mine[:, at]
        out[j, 1 - zh] = other[:, at]


def split_slots(z, mine, other):
    rows, half = mine.shape
    tile = rows_of(rows)
    width = half // 4
    size = 8 * rows * width
    block = pl.BlockSpec((tile, half), lambda i: (i, 0))
    return call(
        split_body,
        (rows // tile,),
        [pl.BlockSpec(memory_space=pltpu.SMEM), block, block],
        pl.BlockSpec((4, 2, tile, width), lambda i: (0, 0, i, 0)),
        jax.ShapeDtypeStruct((4, 2, rows, width), bf16),
        size,
        4 * size,
    )(z, mine, other)


def rounded(v):
    return v.astype(bf16).astype(f32)


def mix_body(step, blocks, wrow, wcol, out):
    count = blocks.shape[2] // step

    @pl.loop(0, count, unroll=2 if count % 2 == 0 else 1)
    def _(t):
        at = pl.ds(pl.multiple_of(t * step, step), step)
        w = wrow[at, :]
        p = [blocks[j % 4, j // 4, at, :].astype(f32) for j in range(8)]
        first = {}
        for zh in range(2):
            for xl in range(2):
                a, b = p[4 * zh + xl], p[4 * zh + 2 + xl]
                first[0, zh, xl] = rounded((a + b) * w[:, zh : zh + 1])
                first[1, zh, xl] = rounded((a - b) * w[:, 2 + zh : 3 + zh])
        for xh in range(2):
            for zh in range(2):
                scale = w[:, 4 + 2 * xh + zh : 5 + 2 * xh + zh]
                g = []
                for xl in range(2):
                    a, b = first[xh, 0, xl], first[xh, 1, xl]
                    g.append(rounded((a + b if zh == 0 else a - b) * scale))
                out[2 * xh, zh, at, :] = ((g[0] + g[1]) * wcol[0:1, :]).astype(bf16)
                out[2 * xh + 1, zh, at, :] = ((g[0] - g[1]) * wcol[1:2, :]).astype(bf16)


def mix(blocks, wrow, wcol, k):
    _, _, rows, width = blocks.shape
    tile = rows_of(rows)
    big = pl.BlockSpec((4, 2, tile, width), lambda i: (0, 0, i, 0))
    size = 8 * rows * width
    return call(
        functools.partial(mix_body, sub_rows(tile)),
        (rows // tile,),
        [big, pl.BlockSpec((tile, 8), lambda i: (i, 0)), pl.BlockSpec((None, 8, width), lambda i: (k, 0, 0))],
        big,
        jax.ShapeDtypeStruct(blocks.shape, bf16),
        8 * size,
        4 * size,
    )(blocks, wrow, wcol)


def inner_body(step, mine, partner, wcol, out):
    count = mine.shape[2] // step

    @pl.loop(0, count, unroll=2 if count % 2 == 0 else 1)
    def _(t):
        at = pl.ds(pl.multiple_of(t * step, step), step)
        for j in range(4):
            for zh in range(2):
                v = mine[j, zh, at, :].astype(f32) * wcol[4:5, :] + partner[j, zh, at, :].astype(f32)
                out[j, zh, at, :] = (v * wcol[2 + j % 2 : 3 + j % 2, :]).astype(bf16)


def inner(mine, partner, wcol, k):
    _, _, rows, width = mine.shape
    tile = rows_of(rows)
    big = pl.BlockSpec((4, 2, tile, width), lambda i: (0, 0, i, 0))
    size = 8 * rows * width
    return call(
        functools.partial(inner_body, sub_rows(tile)),
        (rows // tile,),
        [big, big, pl.BlockSpec((None, 8, width), lambda i: (k, 0, 0))],
        big,
        jax.ShapeDtypeStruct(mine.shape, bf16),
        4 * size,
        6 * size,
    )(mine, partner, wcol)


def factor_body(step, p0, p1, p2, p3, wrow, out):
    count = wrow.shape[0] // step

    @pl.loop(0, count)
    def _(t):
        at = pl.ds(pl.multiple_of(t * step, step), step)
        w = wrow[at, :]
        p = [v[at, :].astype(f32) for v in (p0, p1, p2, p3)]
        for xh in range(2):
            f = []
            for ez in range(2):
                v = p[ez] + p[2 + ez] if xh == 0 else p[ez] - p[2 + ez]
                f.append(v * w[:, 2 * xh + ez : 2 * xh + ez + 1])
            for zh in range(2):
                v = f[0] + f[1] if zh == 0 else f[0] - f[1]
                out[xh, zh, at, :] = (v * w[:, 4 + 2 * xh + zh : 5 + 2 * xh + zh]).astype(bf16)


def factor(pieces, wrow):
    rows, panel = pieces[0].shape
    tile = small_rows_of(rows)
    size = 4 * rows * panel
    return call(
        functools.partial(factor_body, sub_rows(tile)),
        (rows // tile,),
        [pl.BlockSpec((tile, panel), lambda i: (i, 0))] * 4 + [pl.BlockSpec((tile, 8), lambda i: (i, 0))],
        pl.BlockSpec((2, 2, tile, panel), lambda i: (0, 0, i, 0)),
        jax.ShapeDtypeStruct((2, 2, rows, panel), bf16),
        5 * size,
        4 * size,
    )(*pieces, wrow)


def update_body(place, full, mine, passed_left, own, hop1, hop2, hop3, out, top):
    width = full.shape[3]

    @pl.when(pl.program_id(0) == 0)
    def _():
        passed = hop1[...] + hop2[...] + hop3[...]
        top[...] = jnp.where(place[0] == 0, own[...], passed)

    for zh in range(2):
        for xh in range(2):
            left = jnp.where(place[1] == 0, mine[xh, zh], passed_left[xh, zh])
            d = jnp.dot(left, top[...], preferred_element_type=f32)
            for xl in range(2):
                j = 2 * xh + xl
                out[j, zh] = (full[j, zh].astype(f32) - d[:, xl * width : (xl + 1) * width]).astype(bf16)


def update(place, full, left, tops):
    _, _, rows, width = full.shape
    panel = left[0].shape[-1]
    tile = small_rows_of(rows)
    big = pl.BlockSpec((4, 2, tile, width), lambda i: (0, 0, i, 0))
    size = 8 * rows * width
    return pl.pallas_call(
        update_body,
        grid=(rows // tile,),
        in_specs=[
            pl.BlockSpec(memory_space=pltpu.SMEM),
            big,
            *[pl.BlockSpec((2, 2, tile, panel), lambda i: (0, 0, i, 0))] * 2,
            *[pl.BlockSpec((panel, 2 * width), lambda i: (0, 0))] * 4,
        ],
        out_specs=big,
        out_shape=jax.ShapeDtypeStruct(full.shape, bf16),
        scratch_shapes=[pltpu.VMEM((panel, 2 * width), bf16)],
        cost_estimate=pl.CostEstimate(
            flops=2 * size * panel, bytes_accessed=4 * size + 8 * rows * panel, transcendentals=0
        ),
        compiler_params=pltpu.CompilerParams(vmem_limit_bytes=8 * 1024 * 1024),
        name="update",
    )(place, full, *left, *tops)


def gather_body(z, slots, keep, away):
    zh = z[0]
    width = slots.shape[3]
    for j in range(4):
        at = slice(j * width, (j + 1) * width)
        keep[:, at] = slots[j, zh]
        away[:, at] = slots[j, 1 - zh]


def gather_slots(z, slots):
    _, _, rows, width = slots.shape
    tile = rows_of(rows)
    out = pl.BlockSpec((tile, 4 * width), lambda i: (i, 0))
    size = 8 * rows * width
    return call(
        gather_body,
        (rows // tile,),
        [pl.BlockSpec(memory_space=pltpu.SMEM), pl.BlockSpec((4, 2, tile, width), lambda i: (0, 0, i, 0))],
        [out] * 2,
        [jax.ShapeDtypeStruct((rows, 4 * width), bf16)] * 2,
        size,
        4 * size,
    )(z, slots)


def place_body(z, keep, got, *refs):
    out = refs[-1]
    half = keep.shape[1]
    zh = z[0]
    out[:, pl.ds(pl.multiple_of(zh * half, half), half)] = keep[...]
    out[:, pl.ds(pl.multiple_of((1 - zh) * half, half), half)] = got[...]


def place(z, keep, got, whole, k, columns):
    rows, half = keep.shape
    tile = rows_of(rows)
    piece = pl.BlockSpec((tile, half), lambda i: (i, 0))
    ins, args, aliases = [pl.BlockSpec(memory_space=pltpu.SMEM), piece, piece], [z, keep, got], {}
    if whole is not None:
        ins.append(pl.BlockSpec(memory_space=pl.ANY))
        args.append(whole)
        aliases = {3: 0}
    return call(
        place_body,
        (rows // tile,),
        ins,
        pl.BlockSpec((tile, 2 * half), lambda i: (i, k)),
        jax.ShapeDtypeStruct((rows, columns), bf16),
        rows * half,
        8 * rows * half,
        aliases,
    )(*args)


def flip(x, axis):
    return lax.ppermute(x, axis, [(0, 1), (1, 0)])


def trade(x):
    return lax.all_to_all(x, X4, 0, 0, tiled=True)


def steps(system, row_outer, row_inner, col_outer, col_inner, diag_inverse):
    rows, cols = system.shape
    panel = diag_inverse.shape[0]
    width = panel // 4
    chunks = cols // (8 * width)
    xh, xl = lax.axis_index("xh"), lax.axis_index("xl")
    zh, zl = lax.axis_index("zh"), lax.axis_index("zl")
    yh = lax.axis_index("yh")
    y, core = 2 * yh + lax.axis_index("yl"), lax.axis_index("core")

    wr = jnp.stack([row_outer, row_inner]) * root_half
    wr = jnp.stack([wr, flip(wr, "zh")])
    half = 4 * width
    z = zh.reshape(1)
    halves = lambda k, which: lax.dynamic_slice(system, (0, (2 * k + which) * half), (rows, half))
    arrived = []
    for k in range(chunks):
        other = flip(halves(k, 1 - zh), "zh")
        slots = split_slots(z, halves(k, zh), other)
        arrived.append(trade(slots))

    sign_x = (1 - 2 * xh).astype(f32)
    sign_z = (1 - 2 * zh).astype(f32)
    sign_y = (1 - 2 * yh).astype(f32)
    wx = lax.ppermute(wr, "xh", [(0, 1), (1, 0)])
    wr = jnp.stack([jnp.where(xh == 0, wr, wx), jnp.where(xh == 0, wx, wr)])
    near_outer = wr[:, :, 0]
    wr = jnp.where(zh == 0, wr, wr[:, ::-1])
    wrow = jnp.concatenate([wr[:, :, 0].reshape(4, rows), wr[:, :, 1].reshape(4, rows)]).T
    flips = jnp.stack([sign_x * 0 + 1, sign_z])
    wrel = jnp.concatenate(
        [near_outer[0], near_outer[1] * sign_x, wr[0, :, 1] * flips[:, None], wr[1, :, 1] * flips[:, None]]
    ).T
    wc = jnp.stack([col_outer, col_inner]) * root_half
    wc = wc.reshape(2, chunks, 2, 4, width)
    wc = jnp.stack([wc, flip(wc, "xl")])
    wc = jnp.where(xl == 0, wc, wc[::-1])
    wc = lax.dynamic_index_in_dim(wc, zh, 3, keepdims=False)
    wc = lax.dynamic_index_in_dim(wc, 2 * xh + xl, 3, keepdims=False)
    ones = jnp.ones((chunks, width), f32)
    wcol = jnp.stack([wc[0, 0], wc[1, 0], wc[0, 1], wc[1, 1], ones * sign_y, ones, ones, ones], axis=1)

    lead = system[:, :panel].astype(f32)
    lead = (
        (lead + lax.ppermute(system[:, :panel], COLS, [(8, 0), (12, 4)]).astype(f32)) * (col_outer[:panel] * root_half)
    ).astype(bf16)
    lead = (
        (lead.astype(f32) + lax.ppermute(lead, COLS, [(4, 0)]).astype(f32)) * (col_inner[:panel] * root_half)
    ).astype(bf16)
    lead = jnp.dot(lead, diag_inverse, preferred_element_type=f32).astype(bf16)
    near = [lax.ppermute(lead, COLS, [(0, 2 * d)]) for d in (1, 3, 2)]
    lead = jnp.where(y == 0, lead, near[0] + near[1] + near[2])
    lead = jnp.where(xl == 0, lead, lax.ppermute(lead, ("xl", "core"), [(0, 2)]))
    both = [(0, 2), (2, 0)]
    other_z = lax.ppermute(lead, ("zh", "core"), both)
    direct = [lead, other_z] + [lax.ppermute(v, ("xh", "core"), both) for v in (lead, other_z)]
    left = factor(direct, wrel)
    left = [left, flip(left, "core")]
    place_of = jnp.stack([zl, core])

    whole = None
    for k in range(chunks):
        mixed = mix(arrived[k], wrow, wcol, k)
        top = jnp.concatenate([mixed[0, 0, :panel], mixed[1, 0, :panel]], axis=1)
        top_scale = jnp.concatenate([wcol[k, 2], wcol[k, 3]])
        top = top.astype(f32) * sign_y + flip(top, "yh").astype(f32)
        top = (top * top_scale).astype(bf16)
        partner = flip(mixed, "yh")
        full = inner(mixed, partner, wcol, k)
        hops = [lax.ppermute(top, "zl", [(0, d)]) for d in (1, 2, 3)]
        done = update(place_of, full, left, [top] + hops)
        done = trade(done)
        keep, away = gather_slots(z, done)
        got = flip(away, "zh")
        whole = place(z, keep, got, whole, k, cols)
    return whole


def solution(mesh):
    fine = Mesh(
        mesh.devices.reshape(2, 2, 4, 2, 2, 2, 2), ("xh", "zh", "zl", "xl", "yh", "yl", "core")
    )
    prow, pcol = ("xh", "zh", "zl"), ("xl", "yh", "yl", "core")
    in_specs = (P(prow, pcol), P(prow), P(prow), P(pcol), P(pcol), P())
    return jax.shard_map(steps, mesh=fine, in_specs=in_specs, out_specs=P(prow, pcol), check_vma=False)
```

time: 932 us -> 536 us (0.58)
  waiting for transfers between devices: 850 us -> 205 us
  starting transfers between devices: 13 us -> 184 us
  Pallas kernels: 0 us -> 95.9 us
  local copies, waits for them, and re-layouts: 2.71 us -> 29.3 us
  other arithmetic: 37.8 us -> 13.6 us
  between operations: 14.9 us -> 0.76 us
  matrix products: 13 us -> 1.46 us
    ppermute x4 -> x41, waiting for transfers between devices: 675 us -> 204 us  [the longest x19 140 us: flip(): return lax.ppermute(x, axis, [(0, 1), (1, 0)])]
    psum x1 -> x0, waiting for transfers between devices: 175 us -> none  [per_device(): top_rows = lax.psum(term.astype(jnp.bfloat16), 'prow')]
    ppermute x4 -> x41, starting transfers between devices: 12.9 us -> 150 us  [the longest x1 51.1 us: steps(): other_z = lax.ppermute(lead, ('zh', 'core'), both)]
    pallas_call x0 -> x25, Pallas kernels: none -> 95.9 us  [the longest x4 24.5 us: update(): pl.pallas_call(update_body, grid=(rows // tile,), in_specs=[pl.BlockSpec(...]
    convert_element_type x5, other arithmetic: 37.8 us -> 2.49 us  [the longest x1 1.37 us: steps(): lead = ((lead + lax.ppermute(system[:, :panel], COLS, [(8, 0), (12, 4)])....]
    all_to_all x0 -> x8, starting transfers between devices: none -> 34.1 us  [trade(): return lax.all_to_all(x, X4, 0, 0, tiled=True)]
    dot_general x2 -> x1, matrix products: 13 us -> 1.46 us  [steps(): lead = jnp.dot(lead, diag_inverse, preferred_element_type=f32).astype(bf16)]
  transfers between devices with their start and end apart: 6 -> 49, of which waited for: 5 -> 20; matrix products, arithmetic and copies ran while one was open for 0% -> 5% of each run, Pallas kernels for 0% -> 18%
where the time goes in v2:
time: 536 us; the launch traced here: 530 us
  waiting for transfers between devices  205 us (38%)
  starting transfers between devices  184 us (34%)
  Pallas kernels  95.9 us (18%)
  local copies, waits for them, and re-layouts  29.3 us (5%)
  other arithmetic  13.6 us (3%)
    ppermute x19, waiting for transfers between devices, flip(): return lax.ppermute(x, axis, [(0, 1), (1, 0)])  140 us
    ppermute x1, starting transfers between devices, steps(): other_z = lax.ppermute(lead, ('zh', 'core'), both)  51.1 us
    ppermute x19, starting transfers between devices, flip(): return lax.ppermute(x, axis, [(0, 1), (1, 0)])  48.8 us
    all_to_all x8, starting transfers between devices, trade(): return lax.all_to_all(x, X4, 0, 0, tiled=True)  34.1 us
    ppermute x3, waiting for transfers between devices, steps(): near = [lax.ppermute(lead, COLS, [(0, 2 * d)]) for d in (1, 3, 2)]  33.4 us
    ppermute x12, starting transfers between devices, steps(): hops = [lax.ppermute(top, 'zl', [(0, d)]) for d in (1, 2, 3)]  28.7 us
    pallas_call x4, Pallas kernels, update(): pl.pallas_call(update_body, grid=(rows // tile,), in_specs=[pl.BlockSpec(...  24.5 us
    ppermute x12, waiting for transfers between devices, steps(): hops = [lax.ppermute(top, 'zl', [(0, d)]) for d in (1, 2, 3)]  22.7 us
  transfers between devices with their start and end apart: 49, of which 20 were waited for; matrix products, arithmetic and copies ran while one was open for 5% of the time, Pallas kernels for 18%

profile of v2, /device:TPU:24, one launch (start us, length us, event | category | flops | bytes accessed | tf_op | source)
XLA Modules:
  0.0 530.5 jit_solution(12461184290351063595)
XLA Ops:
  0.0 5.4 %constant_dynamic-slice_fusion = (bf16[768,512]{1,0:T(8,128)(2,1)}, bf16[768,512]{1,0:T(8,128)(2,1)}, bf16[768,512]{1,0:T(8,128)(2,1)}, bf16[768,512]{1,0:T(8,12...) fusion(bf16[768,4096]{1,0:T(8,128)(2,1)} %param.6, ...), kind=kLoop, calls=%fused_computation.46 | loop fusion | bytes 14155808 | tf_op jit(solution)/shard_map/dynamic_slice | solution.py:295
  14.9 7.3 %collective-permute-start = (bf16[768,512]{1,0:T(8,128)(2,1)}, bf16[768,512]{1,0:T(8,128)(2,1)S(1)}, u32[]{:S(2)}, u32[]{:S(2)}) collective-permute-start(bf16[768,512]{1,0:T(8,128)(2,1)} %get-tuple-element.29), channel_id=1, source_target_pairs={{0,64},{64,0},{1,65},{65,1},{2,66},{66,2},{3,67},{67,3},{4,68},{68... | collective-permute-start | bytes 2359304 | tf_op jit(solution)/shard_map/ppermute | solution.py:274
  22.2 33.4 %collective-permute-done.8 = bf16[768,512]{1,0:T(8,128)(2,1)} collective-permute-done((bf16[768,512]{1,0:T(8,128)(2,1)}, bf16[768,512]{1,0:T(8,128)(2,1)}, u32[]{:S(2)}, u32[]{:S(2)}) %collective-permute-start.8) | collective-permute-done | bytes 786464 | tf_op jit(solution)/shard_map/ppermute | solution.py:331
  60.5 5.6 %collective-permute-start.1 = (f32[2,768]{1,0:T(2,128)S(1)}, f32[2,768]{1,0:T(2,128)S(1)}, u32[]{:S(2)}, u32[]{:S(2)}) collective-permute-start(f32[2,768]{1,0:T(2,128)S(1)} %maximum_multiply_fusion.3), channel_id=1, source_target_pairs={{0,64},{64,0},{1,65},{65,1},{2,66},{66,2},{3,67},{67,3},{4,68},{68... | collective-permute-start | bytes 18440 | tf_op jit(solution)/shard_map/ppermute | solution.py:274
  66.5 5.5 %collective-permute-start.27 = (bf16[768,512]{1,0:T(8,128)(2,1)}, bf16[768,512]{1,0:T(8,128)(2,1)}, u32[]{:S(2)}, u32[]{:S(2)}) collective-permute-start(bf16[768,512]{1,0:T(8,128)(2,1)} %get-tuple-element.24), channel_id=1, source_target_pairs={{0,64},{64,0},{1,65},{65,1},{2,66},{66,2},{3,67},{67,3},{4,68},{68... | collective-permute-start | bytes 2359304 | tf_op jit(solution)/shard_map/ppermute | solution.py:274
  77.0 3.6 all-to-all-start
  81.8 51.1 %collective-permute-start.11 = (bf16[768,512]{1,0:T(8,128)(2,1)S(1)}, bf16[768,512]{1,0:T(8,128)(2,1)}, u32[]{:S(2)}, u32[]{:S(2)}) collective-permute-start(bf16[768,512]{1,0:T(8,128)(2,1)S(1)} %broadcast_select_fusion.p0), channel_id=1, source_target_pairs={{0,64},{64,0},{2,66},{66,2},{4,68},{68,4},{6,70},{70,6},{8,72},{72... | collective-permute-start | bytes 2359304 | tf_op jit(solution)/shard_map/ppermute | solution.py:335
  133.1 5.4 %collective-permute-start.12 = (bf16[768,512]{1,0:T(8,128)(2,1)S(1)}, bf16[768,512]{1,0:T(8,128)(2,1)}, u32[]{:S(2)}, u32[]{:S(2)}) collective-permute-start(bf16[768,512]{1,0:T(8,128)(2,1)S(1)} %broadcast_select_fusion.p0), channel_id=1, source_target_pairs={{0,128},{128,0},{2,130},{130,2},{4,132},{132,4},{6,134},{134,6},{8... | collective-permute-start | bytes 2359304 | tf_op jit(solution)/shard_map/ppermute | solution.py:336
  138.4 7.0 %collective-permute-done.11.p1 = bf16[768,512]{1,0:T(8,128)(2,1)} collective-permute-done((bf16[768,512]{1,0:T(8,128)(2,1)S(1)}, bf16[768,512]{1,0:T(8,128)(2,1)}, u32[]{:S(2)}, u32[]{:S(2)}) %collective-permute-start.11) | collective-permute-done | bytes 786464 | tf_op jit(solution)/shard_map/ppermute | solution.py:335
  145.4 5.0 collective-permute-start.13
  150.4 3.6 shard_map.69
  155.1 4.4 all-to-all-start.2
  162.2 7.1 %shard_map.67.mine = bf16[2,2,768,512]{3,2,1,0:T(8,128)(2,1)S(1)} custom-call(bf16[768,512]{1,0:T(8,128)(2,1)S(1)} %copy-done.11, bf16[768,512]{1,0:T(8,128)(2,1)} %collective-permute-done.11.p1, bf16[768,512]{1,0:T(8,128)(2,1)} %collective-permute-done.12.p2, bf16[768,512]{1,0:T(8,128)(2,1)} %collective-permute-done.13.p3, f32[768,8]{1,0:T(8,128)S(1)} %bitcast.75), custom_call_target="tpu_custom_call" | custom-call | flops 7864320 | bytes 6291456 | tf_op jit(solution)/shard_map/pallas_call | solution.py:165
  171.4 4.2 collective-permute-start.34
  182.4 4.4 all-to-all-start.4
  195.1 5.3 shard_map.70.mine
  200.4 3.4 collective-permute-done.34.other
  207.9 4.3 all-to-all-start.6
  215.3 5.2 shard_map.74.mine
  223.5 21.5 %collective-permute-done.22 = bf16[512,256]{1,0:T(8,128)(2,1)S(1)} collective-permute-done((bf16[512,256]{1,0:T(8,128)(2,1)S(1)}, bf16[512,256]{1,0:T(8,128)(2,1)S(1)}, u32[]{:S(2)}, u32[]{:S(2)}) %collective-permute-start.22) | collective-permute-done | bytes 262176 | tf_op jit(solution)/shard_map/ppermute | solution.py:274
  254.9 4.8 collective-permute-done.24.hop2
  262.7 6.4 %update.5 = bf16[4,2,768,128]{3,2,1,0:T(8,128)(2,1)S(1)} custom-call(s32[2]{0:T(128)S(1)} %pad_add_fusion.place, bf16[4,2,768,128]{3,2,1,0:T(8,128)(2,1)S(1)} %shard_map.71.full, bf16[2,2,768,512]{3,2,1,0:T(8,128)(2,1)S(1)} %shard_map.67.mine, bf16[2,2,768,512]{3,2,1,0:T(8,128)(2,1)} %collective-permute-done.14.passed_left, ...), custom_call_target="tpu_custom_call" | custom-call | flops 805306368 | bytes 6291456 | tf_op jit(solution)/shard_map/update/pallas_call | solution.py:199
  270.3 4.5 all-to-all-start.3
  277.5 5.2 shard_map.78.mine
  289.6 3.5 collective-permute-start.32
  300.9 6.0 %update.6 = bf16[4,2,768,128]{3,2,1,0:T(8,128)(2,1)S(1)} custom-call(s32[2]{0:T(128)S(1)} %copy-done.17, bf16[4,2,768,128]{3,2,1,0:T(8,128)(2,1)S(1)} %shard_map.75.full, bf16[2,2,768,512]{3,2,1,0:T(8,128)(2,1)S(1)} %shard_map.67.mine, bf16[2,2,768,512]{3,2,1,0:T(8,128)(2,1)} %collective-permute-done.14.passed_left, ...), custom_call_target="tpu_custom_call" | custom-call | flops 805306368 | bytes 6291456 | tf_op jit(solution)/shard_map/update/pallas_call | solution.py:199
  308.2 4.5 all-to-all-start.5
  316.8 3.9 shard_map.65.mine
  326.6 3.9 collective-permute-start.38
  340.1 6.0 %update.7 = bf16[4,2,768,128]{3,2,1,0:T(8,128)(2,1)S(1)} custom-call(s32[2]{0:T(128)S(1)} %copy-done.18, bf16[4,2,768,128]{3,2,1,0:T(8,128)(2,1)S(1)} %shard_map.79.full, bf16[2,2,768,512]{3,2,1,0:T(8,128)(2,1)S(1)} %shard_map.67.mine, bf16[2,2,768,512]{3,2,1,0:T(8,128)(2,1)} %collective-permute-done.14.passed_left, ...), custom_call_target="tpu_custom_call" | custom-call | flops 805306368 | bytes 6291456 | tf_op jit(solution)/shard_map/update/pallas_call | solution.py:199
  347.3 4.3 all-to-all-start.7
  354.3 8.3 %collective-permute-done.15 = bf16[512,256]{1,0:T(8,128)(2,1)S(1)} collective-permute-done((bf16[512,256]{1,0:T(8,128)(2,1)S(1)}, bf16[512,256]{1,0:T(8,128)(2,1)S(1)}, u32[]{:S(2)}, u32[]{:S(2)}) %collective-permute-start.15) | collective-permute-done | bytes 262176 | tf_op jit(solution)/shard_map/ppermute | solution.py:274
  365.6 4.5 collective-permute-start.18
  376.2 3.1 collective-permute-done.18.hop3
  379.4 6.0 %update.4 = bf16[4,2,768,128]{3,2,1,0:T(8,128)(2,1)S(1)} custom-call(s32[2]{0:T(128)S(1)} %copy-done.18, bf16[4,2,768,128]{3,2,1,0:T(8,128)(2,1)S(1)} %shard_map.66.full, bf16[2,2,768,512]{3,2,1,0:T(8,128)(2,1)S(1)} %shard_map.67.mine, bf16[2,2,768,512]{3,2,1,0:T(8,128)(2,1)} %collective-permute-done.14.passed_left, ...), custom_call_target="tpu_custom_call" | custom-call | flops 805306368 | bytes 6291456 | tf_op jit(solution)/shard_map/update/pallas_call | solution.py:199
  386.6 4.1 all-to-all-start.1
  390.7 3.5 shard_map.80
  396.2 3.5 shard_map.76
  399.7 3.9 collective-permute-start.33
  403.6 3.5 shard_map.72
  409.6 4.0 collective-permute-start.19
  413.7 64.8 %collective-permute-done.40.got = bf16[768,512]{1,0:T(8,128)(2,1)} collective-permute-done((bf16[768,512]{1,0:T(8,128)(2,1)}, bf16[768,512]{1,0:T(8,128)(2,1)}, u32[]{:S(2)}, u32[]{:S(2)}) %collective-permute-start.40) | collective-permute-done | bytes 786464 | tf_op jit(solution)/shard_map/ppermute | solution.py:274
  478.4 3.4 shard_map.81.refs_0_
  481.9 13.4 %collective-permute-done.33.got = bf16[768,512]{1,0:T(8,128)(2,1)} collective-permute-done((bf16[768,512]{1,0:T(8,128)(2,1)}, bf16[768,512]{1,0:T(8,128)(2,1)}, u32[]{:S(2)}, u32[]{:S(2)}) %collective-permute-start.33) | collective-permute-done | bytes 786464 | tf_op jit(solution)/shard_map/ppermute | solution.py:274
  495.3 3.4 shard_map.82.refs_0_
  498.7 13.4 %collective-permute-done.26.got = bf16[768,512]{1,0:T(8,128)(2,1)} collective-permute-done((bf16[768,512]{1,0:T(8,128)(2,1)}, bf16[768,512]{1,0:T(8,128)(2,1)}, u32[]{:S(2)}, u32[]{:S(2)}) %collective-permute-start.26) | collective-permute-done | bytes 786464 | tf_op jit(solution)/shard_map/ppermute | solution.py:274
  512.2 3.4 shard_map.83.refs_0_
  515.6 13.2 %collective-permute-done.19.got = bf16[768,512]{1,0:T(8,128)(2,1)S(1)} collective-permute-done((bf16[768,512]{1,0:T(8,128)(2,1)S(1)}, bf16[768,512]{1,0:T(8,128)(2,1)S(1)}, u32[]{:S(2)}, u32[]{:S(2)}) %collective-permute-start.19) | collective-permute-done | bytes 786464 | tf_op jit(solution)/shard_map/ppermute | solution.py:274
  (187 shorter events, 124.6 us)
Async XLA Ops:
  5.4 1.5 collective-permute-start.5
  10.5 11.7 %collective-permute-start.9 = (bf16[768,512]{1,0:T(8,128)(2,1)}, bf16[768,512]{1,0:T(8,128)(2,1)}, u32[]{:S(2)}, u32[]{:S(2)}) collective-permute-start(bf16[768,512]{1,0:T(8,128)(2,1)} %convolution_convert_fusion), channel_id=1, source_target_pairs={{0,4},{16,20},{32,36},{48,52},{64,68},{80,84},{96,100},{112,116},{... | collective-permute-start | bytes 2359304 | tf_op jit(solution)/shard_map/ppermute | solution.py:331
  12.1 10.1 %collective-permute-start.7 = (bf16[768,512]{1,0:T(8,128)(2,1)}, bf16[768,512]{1,0:T(8,128)(2,1)}, u32[]{:S(2)}, u32[]{:S(2)}) collective-permute-start(bf16[768,512]{1,0:T(8,128)(2,1)} %convolution_convert_fusion), channel_id=1, source_target_pairs={{0,2},{16,18},{32,34},{48,50},{64,66},{80,82},{96,98},{112,114},{1... | collective-permute-start | bytes 2359304 | tf_op jit(solution)/shard_map/ppermute | solution.py:331
  13.7 42.0 %collective-permute-start.8 = (bf16[768,512]{1,0:T(8,128)(2,1)}, bf16[768,512]{1,0:T(8,128)(2,1)}, u32[]{:S(2)}, u32[]{:S(2)}) collective-permute-start(bf16[768,512]{1,0:T(8,128)(2,1)} %convolution_convert_fusion), channel_id=1, source_target_pairs={{0,6},{16,22},{32,38},{48,54},{64,70},{80,86},{96,102},{112,118},{... | collective-permute-start | bytes 2359304 | tf_op jit(solution)/shard_map/ppermute | solution.py:331
  14.9 60.3 %collective-permute-start = (bf16[768,512]{1,0:T(8,128)(2,1)}, bf16[768,512]{1,0:T(8,128)(2,1)S(1)}, u32[]{:S(2)}, u32[]{:S(2)}) collective-permute-start(bf16[768,512]{1,0:T(8,128)(2,1)} %get-tuple-element.29), channel_id=1, source_target_pairs={{0,64},{64,0},{1,65},{65,1},{2,66},{66,2},{3,67},{67,3},{4,68},{68... | collective-permute-start | bytes 2359304 | tf_op jit(solution)/shard_map/ppermute | solution.py:274
  58.3 22.3 %collective-permute-start.10 = (bf16[768,512]{1,0:T(8,128)(2,1)}, bf16[768,512]{1,0:T(8,128)(2,1)}, u32[]{:S(2)}, u32[]{:S(2)}) collective-permute-start(bf16[768,512]{1,0:T(8,128)(2,1)} %add_select_fusion), channel_id=1, source_target_pairs={{0,8},{2,10},{4,12},{6,14},{16,24},{18,26},{20,28},{22,30},{32,40}... | collective-permute-start | bytes 2359304 | tf_op jit(solution)/shard_map/ppermute | solution.py:333
  60.5 11.6 %collective-permute-start.1 = (f32[2,768]{1,0:T(2,128)S(1)}, f32[2,768]{1,0:T(2,128)S(1)}, u32[]{:S(2)}, u32[]{:S(2)}) collective-permute-start(f32[2,768]{1,0:T(2,128)S(1)} %maximum_multiply_fusion.3), channel_id=1, source_target_pairs={{0,64},{64,0},{1,65},{65,1},{2,66},{66,2},{3,67},{67,3},{4,68},{68... | collective-permute-start | bytes 18440 | tf_op jit(solution)/shard_map/ppermute | solution.py:274
  66.1 84.3 %collective-permute-start.20 = (bf16[768,512]{1,0:T(8,128)(2,1)}, bf16[768,512]{1,0:T(8,128)(2,1)}, u32[]{:S(2)}, u32[]{:S(2)}) collective-permute-start(bf16[768,512]{1,0:T(8,128)(2,1)} %get-tuple-element.26), channel_id=1, source_target_pairs={{0,64},{64,0},{1,65},{65,1},{2,66},{66,2},{3,67},{67,3},{4,68},{68... | collective-permute-start | bytes 2359304 | tf_op jit(solution)/shard_map/ppermute | solution.py:274
  66.5 111.3 %collective-permute-start.27 = (bf16[768,512]{1,0:T(8,128)(2,1)}, bf16[768,512]{1,0:T(8,128)(2,1)}, u32[]{:S(2)}, u32[]{:S(2)}) collective-permute-start(bf16[768,512]{1,0:T(8,128)(2,1)} %get-tuple-element.24), channel_id=1, source_target_pairs={{0,64},{64,0},{1,65},{65,1},{2,66},{66,2},{3,67},{67,3},{4,68},{68... | collective-permute-start | bytes 2359304 | tf_op jit(solution)/shard_map/ppermute | solution.py:274
  72.1 60.8 %collective-permute-start.2 = (f32[2,2,768]{2,1,0:T(2,128)S(1)}, f32[2,2,768]{2,1,0:T(2,128)S(1)}, u32[]{:S(2)}, u32[]{:S(2)}) collective-permute-start(f32[2,2,768]{2,1,0:T(2,128)S(1)} %pad_maximum_fusion.8), channel_id=1, source_target_pairs={{0,128},{128,0},{1,129},{129,1},{2,130},{130,2},{3,131},{131,3},{4... | collective-permute-start | bytes 36872 | tf_op jit(solution)/shard_map/ppermute | solution.py:305
  77.0 77.0 %all-to-all-start = ((bf16[4,2,768,128]{3,2,1,0:T(8,128)(2,1)}), bf16[4,2,768,128]{3,2,1,0:T(8,128)(2,1)S(1)}, u32[]{:S(2)}, u32[]{:S(2)}) async-start(bf16[4,2,768,128]{3,2,1,0:T(8,128)(2,1)} %shard_map.64), calls=%async_computation | async-start | bytes 3145728 | tf_op jit(solution)/shard_map/all_to_all | solution.py:278
  81.8 63.6 %collective-permute-start.11 = (bf16[768,512]{1,0:T(8,128)(2,1)S(1)}, bf16[768,512]{1,0:T(8,128)(2,1)}, u32[]{:S(2)}, u32[]{:S(2)}) collective-permute-start(bf16[768,512]{1,0:T(8,128)(2,1)S(1)} %broadcast_select_fusion.p0), channel_id=1, source_target_pairs={{0,64},{64,0},{2,66},{66,2},{4,68},{68,4},{6,70},{70,6},{8,72},{72... | collective-permute-start | bytes 2359304 | tf_op jit(solution)/shard_map/ppermute | solution.py:335
  133.1 26.7 %collective-permute-start.12 = (bf16[768,512]{1,0:T(8,128)(2,1)S(1)}, bf16[768,512]{1,0:T(8,128)(2,1)}, u32[]{:S(2)}, u32[]{:S(2)}) collective-permute-start(bf16[768,512]{1,0:T(8,128)(2,1)S(1)} %broadcast_select_fusion.p0), channel_id=1, source_target_pairs={{0,128},{128,0},{2,130},{130,2},{4,132},{132,4},{6,134},{134,6},{8... | collective-permute-start | bytes 2359304 | tf_op jit(solution)/shard_map/ppermute | solution.py:336
  145.4 15.7 %collective-permute-start.13 = (bf16[768,512]{1,0:T(8,128)(2,1)}, bf16[768,512]{1,0:T(8,128)(2,1)}, u32[]{:S(2)}, u32[]{:S(2)}) collective-permute-start(bf16[768,512]{1,0:T(8,128)(2,1)} %collective-permute-done.11.p1), channel_id=1, source_target_pairs={{0,128},{128,0},{2,130},{130,2},{4,132},{132,4},{6,134},{134,6},{8... | collective-permute-start | bytes 2359304 | tf_op jit(solution)/shard_map/ppermute | solution.py:336
  155.1 27.3 %all-to-all-start.2 = ((bf16[4,2,768,128]{3,2,1,0:T(8,128)(2,1)}), bf16[4,2,768,128]{3,2,1,0:T(8,128)(2,1)}, u32[]{:S(2)}, u32[]{:S(2)}) async-start(bf16[4,2,768,128]{3,2,1,0:T(8,128)(2,1)} %shard_map.69), calls=%async_computation.2 | async-start | bytes 3145728 | tf_op jit(solution)/shard_map/all_to_all | solution.py:278
  169.3 93.3 %collective-permute-start.14 = (bf16[2,2,768,512]{3,2,1,0:T(8,128)(2,1)S(1)}, bf16[2,2,768,512]{3,2,1,0:T(8,128)(2,1)}, u32[]{:S(2)}, u32[]{:S(2)}) collective-permute-start(bf16[2,2,768,512]{3,2,1,0:T(8,128)(2,1)S(1)} %shard_map.67.mine), channel_id=1, source_target_pairs={{0,1},{1,0},{2,3},{3,2},{4,5},{5,4},{6,7},{7,6},{8,9},{9,8},{10,11... | collective-permute-start | bytes 9437192 | tf_op jit(solution)/shard_map/ppermute | solution.py:274
  170.1 18.2 %collective-permute-start.3 = (f32[2,4,2,4,128]{4,3,2,1,0:T(4,128)}, f32[2,4,2,4,128]{4,3,2,1,0:T(4,128)}, u32[]{:S(2)}, u32[]{:S(2)}) collective-permute-start(f32[2,4,2,4,128]{4,3,2,1,0:T(4,128)} %maximum_multiply_fusion.1), channel_id=1, source_target_pairs={{0,8},{8,0},{1,9},{9,1},{2,10},{10,2},{3,11},{11,3},{4,12},{12,4},... | collective-permute-start | bytes 98312 | tf_op jit(solution)/shard_map/ppermute | solution.py:274
  171.4 32.4 %collective-permute-start.34 = (bf16[768,512]{1,0:T(8,128)(2,1)}, bf16[768,512]{1,0:T(8,128)(2,1)}, u32[]{:S(2)}, u32[]{:S(2)}) collective-permute-start(bf16[768,512]{1,0:T(8,128)(2,1)} %get-tuple-element.23), channel_id=1, source_target_pairs={{0,64},{64,0},{1,65},{65,1},{2,66},{66,2},{3,67},{67,3},{4,68},{68... | collective-permute-start | bytes 2359304 | tf_op jit(solution)/shard_map/ppermute | solution.py:274
  182.4 25.5 %all-to-all-start.4 = ((bf16[4,2,768,128]{3,2,1,0:T(8,128)(2,1)}), bf16[4,2,768,128]{3,2,1,0:T(8,128)(2,1)}, u32[]{:S(2)}, u32[]{:S(2)}) async-start(bf16[4,2,768,128]{3,2,1,0:T(8,128)(2,1)} %copy-done.5), calls=%async_computation.4 | async-start | bytes 3145728 | tf_op jit(solution)/shard_map/all_to_all | solution.py:278
  200.4 49.4 %collective-permute-start.21 = (bf16[4,2,768,128]{3,2,1,0:T(8,128)(2,1)}, bf16[4,2,768,128]{3,2,1,0:T(8,128)(2,1)}, u32[]{:S(2)}, u32[]{:S(2)}) collective-permute-start(bf16[4,2,768,128]{3,2,1,0:T(8,128)(2,1)} %shard_map.70.mine), channel_id=1, source_target_pairs={{0,4},{4,0},{1,5},{5,1},{2,6},{6,2},{3,7},{7,3},{8,12},{12,8},{9,1... | collective-permute-start | bytes 4718600 | tf_op jit(solution)/shard_map/ppermute | solution.py:274
  207.9 62.3 %all-to-all-start.6 = ((bf16[4,2,768,128]{3,2,1,0:T(8,128)(2,1)}), bf16[4,2,768,128]{3,2,1,0:T(8,128)(2,1)}, u32[]{:S(2)}, u32[]{:S(2)}) async-start(bf16[4,2,768,128]{3,2,1,0:T(8,128)(2,1)} %copy-done.4), calls=%async_computation.6 | async-start | bytes 3145728 | tf_op jit(solution)/shard_map/all_to_all | solution.py:278
  213.3 31.7 %collective-permute-start.22 = (bf16[512,256]{1,0:T(8,128)(2,1)S(1)}, bf16[512,256]{1,0:T(8,128)(2,1)S(1)}, u32[]{:S(2)}, u32[]{:S(2)}) collective-permute-start(bf16[512,256]{1,0:T(8,128)(2,1)S(1)} %pad_maximum_fusion.1), channel_id=1, source_target_pairs={{0,4},{4,0},{1,5},{5,1},{2,6},{6,2},{3,7},{7,3},{8,12},{12,8},{9,1... | collective-permute-start | bytes 786440 | tf_op jit(solution)/shard_map/ppermute | solution.py:274
  220.5 72.5 %collective-permute-start.28 = (bf16[4,2,768,128]{3,2,1,0:T(8,128)(2,1)}, bf16[4,2,768,128]{3,2,1,0:T(8,128)(2,1)}, u32[]{:S(2)}, u32[]{:S(2)}) collective-permute-start(bf16[4,2,768,128]{3,2,1,0:T(8,128)(2,1)} %shard_map.74.mine), channel_id=1, source_target_pairs={{0,4},{4,0},{1,5},{5,1},{2,6},{6,2},{3,7},{7,3},{8,12},{12,8},{9,1... | collective-permute-start | bytes 4718600 | tf_op jit(solution)/shard_map/ppermute | solution.py:274
  245.8 9.1 %collective-permute-start.23 = (bf16[512,256]{1,0:T(8,128)(2,1)}, bf16[512,256]{1,0:T(8,128)(2,1)}, u32[]{:S(2)}, u32[]{:S(2)}) collective-permute-start(bf16[512,256]{1,0:T(8,128)(2,1)} %multiply_convert_fusion.5.own), channel_id=1, source_target_pairs={{0,16},{1,17},{2,18},{3,19},{4,20},{5,21},{6,22},{7,23},{8,24},{9,... | collective-permute-start | bytes 786440 | tf_op jit(solution)/shard_map/ppermute | solution.py:350
  247.8 11.9 %collective-permute-start.24 = (bf16[512,256]{1,0:T(8,128)(2,1)}, bf16[512,256]{1,0:T(8,128)(2,1)}, u32[]{:S(2)}, u32[]{:S(2)}) collective-permute-start(bf16[512,256]{1,0:T(8,128)(2,1)} %multiply_convert_fusion.5.own), channel_id=1, source_target_pairs={{0,32},{1,33},{2,34},{3,35},{4,36},{5,37},{6,38},{7,39},{8,40},{9,... | collective-permute-start | bytes 786440 | tf_op jit(solution)/shard_map/ppermute | solution.py:350
  249.8 12.9 %collective-permute-start.25 = (bf16[512,256]{1,0:T(8,128)(2,1)}, bf16[512,256]{1,0:T(8,128)(2,1)}, u32[]{:S(2)}, u32[]{:S(2)}) collective-permute-start(bf16[512,256]{1,0:T(8,128)(2,1)} %multiply_convert_fusion.5.own), channel_id=1, source_target_pairs={{0,48},{1,49},{2,50},{3,51},{4,52},{5,53},{6,54},{7,55},{8,56},{9,... | collective-permute-start | bytes 786440 | tf_op jit(solution)/shard_map/ppermute | solution.py:350
  270.3 37.9 %all-to-all-start.3 = ((bf16[4,2,768,128]{3,2,1,0:T(8,128)(2,1)}), bf16[4,2,768,128]{3,2,1,0:T(8,128)(2,1)}, u32[]{:S(2)}, u32[]{:S(2)}) async-start(bf16[4,2,768,128]{3,2,1,0:T(8,128)(2,1)} %copy-done.7), calls=%async_computation.3 | async-start | bytes 3145728 | tf_op jit(solution)/shard_map/all_to_all | solution.py:278
  275.8 9.5 %collective-permute-start.29 = (bf16[512,256]{1,0:T(8,128)(2,1)S(1)}, bf16[512,256]{1,0:T(8,128)(2,1)S(1)}, u32[]{:S(2)}, u32[]{:S(2)}) collective-permute-start(bf16[512,256]{1,0:T(8,128)(2,1)S(1)} %pad_maximum_fusion.2), channel_id=1, source_target_pairs={{0,4},{4,0},{1,5},{5,1},{2,6},{6,2},{3,7},{7,3},{8,12},{12,8},{9,1... | collective-permute-start | bytes 786440 | tf_op jit(solution)/shard_map/ppermute | solution.py:274
  282.7 50.4 %collective-permute-start.35 = (bf16[4,2,768,128]{3,2,1,0:T(8,128)(2,1)}, bf16[4,2,768,128]{3,2,1,0:T(8,128)(2,1)}, u32[]{:S(2)}, u32[]{:S(2)}) collective-permute-start(bf16[4,2,768,128]{3,2,1,0:T(8,128)(2,1)} %shard_map.78.mine), channel_id=1, source_target_pairs={{0,4},{4,0},{1,5},{5,1},{2,6},{6,2},{3,7},{7,3},{8,12},{12,8},{9,1... | collective-permute-start | bytes 4718600 | tf_op jit(solution)/shard_map/ppermute | solution.py:274
  285.5 10.6 %collective-permute-start.30 = (bf16[512,256]{1,0:T(8,128)(2,1)S(1)}, bf16[512,256]{1,0:T(8,128)(2,1)S(1)}, u32[]{:S(2)}, u32[]{:S(2)}) collective-permute-start(bf16[512,256]{1,0:T(8,128)(2,1)S(1)} %multiply_convert_fusion.4.own), channel_id=1, source_target_pairs={{0,16},{1,17},{2,18},{3,19},{4,20},{5,21},{6,22},{7,23},{8,24},{9,... | collective-permute-start | bytes 786440 | tf_op jit(solution)/shard_map/ppermute | solution.py:350
  286.8 11.3 %collective-permute-start.31 = (bf16[512,256]{1,0:T(8,128)(2,1)S(1)}, bf16[512,256]{1,0:T(8,128)(2,1)S(1)}, u32[]{:S(2)}, u32[]{:S(2)}) collective-permute-start(bf16[512,256]{1,0:T(8,128)(2,1)S(1)} %multiply_convert_fusion.4.own), channel_id=1, source_target_pairs={{0,32},{1,33},{2,34},{3,35},{4,36},{5,37},{6,38},{7,39},{8,40},{9,... | collective-permute-start | bytes 786440 | tf_op jit(solution)/shard_map/ppermute | solution.py:350
  289.6 11.3 %collective-permute-start.32 = (bf16[512,256]{1,0:T(8,128)(2,1)S(1)}, bf16[512,256]{1,0:T(8,128)(2,1)S(1)}, u32[]{:S(2)}, u32[]{:S(2)}) collective-permute-start(bf16[512,256]{1,0:T(8,128)(2,1)S(1)} %multiply_convert_fusion.4.own), channel_id=1, source_target_pairs={{0,48},{1,49},{2,50},{3,51},{4,52},{5,53},{6,54},{7,55},{8,56},{9,... | collective-permute-start | bytes 786440 | tf_op jit(solution)/shard_map/ppermute | solution.py:350
  308.2 39.1 %all-to-all-start.5 = ((bf16[4,2,768,128]{3,2,1,0:T(8,128)(2,1)}), bf16[4,2,768,128]{3,2,1,0:T(8,128)(2,1)}, u32[]{:S(2)}, u32[]{:S(2)}) async-start(bf16[4,2,768,128]{3,2,1,0:T(8,128)(2,1)} %copy-done.6), calls=%async_computation.5 | async-start | bytes 3145728 | tf_op jit(solution)/shard_map/all_to_all | solution.py:278
  313.7 11.5 %collective-permute-start.36 = (bf16[512,256]{1,0:T(8,128)(2,1)S(1)}, bf16[512,256]{1,0:T(8,128)(2,1)S(1)}, u32[]{:S(2)}, u32[]{:S(2)}) collective-permute-start(bf16[512,256]{1,0:T(8,128)(2,1)S(1)} %pad_maximum_fusion.3), channel_id=1, source_target_pairs={{0,4},{4,0},{1,5},{5,1},{2,6},{6,2},{3,7},{7,3},{8,12},{12,8},{9,1... | collective-permute-start | bytes 786440 | tf_op jit(solution)/shard_map/ppermute | solution.py:274
  320.6 49.5 %collective-permute-start.4 = (bf16[4,2,768,128]{3,2,1,0:T(8,128)(2,1)}, bf16[4,2,768,128]{3,2,1,0:T(8,128)(2,1)}, u32[]{:S(2)}, u32[]{:S(2)}) collective-permute-start(bf16[4,2,768,128]{3,2,1,0:T(8,128)(2,1)} %shard_map.65.mine), channel_id=1, source_target_pairs={{0,4},{4,0},{1,5},{5,1},{2,6},{6,2},{3,7},{7,3},{8,12},{12,8},{9,1... | collective-permute-start | bytes 4718600 | tf_op jit(solution)/shard_map/ppermute | solution.py:274
  325.3 10.7 %collective-permute-start.37 = (bf16[512,256]{1,0:T(8,128)(2,1)S(1)}, bf16[512,256]{1,0:T(8,128)(2,1)S(1)}, u32[]{:S(2)}, u32[]{:S(2)}) collective-permute-start(bf16[512,256]{1,0:T(8,128)(2,1)S(1)} %multiply_convert_fusion.3.own), channel_id=1, source_target_pairs={{0,16},{1,17},{2,18},{3,19},{4,20},{5,21},{6,22},{7,23},{8,24},{9,... | collective-permute-start | bytes 786440 | tf_op jit(solution)/shard_map/ppermute | solution.py:350
  326.6 10.6 %collective-permute-start.38 = (bf16[512,256]{1,0:T(8,128)(2,1)S(1)}, bf16[512,256]{1,0:T(8,128)(2,1)S(1)}, u32[]{:S(2)}, u32[]{:S(2)}) collective-permute-start(bf16[512,256]{1,0:T(8,128)(2,1)S(1)} %multiply_convert_fusion.3.own), channel_id=1, source_target_pairs={{0,32},{1,33},{2,34},{3,35},{4,36},{5,37},{6,38},{7,39},{8,40},{9,... | collective-permute-start | bytes 786440 | tf_op jit(solution)/shard_map/ppermute | solution.py:350
  330.6 9.5 %collective-permute-start.39 = (bf16[512,256]{1,0:T(8,128)(2,1)S(1)}, bf16[512,256]{1,0:T(8,128)(2,1)S(1)}, u32[]{:S(2)}, u32[]{:S(2)}) collective-permute-start(bf16[512,256]{1,0:T(8,128)(2,1)S(1)} %multiply_convert_fusion.3.own), channel_id=1, source_target_pairs={{0,48},{1,49},{2,50},{3,51},{4,52},{5,53},{6,54},{7,55},{8,56},{9,... | collective-permute-start | bytes 786440 | tf_op jit(solution)/shard_map/ppermute | solution.py:350
  347.3 39.3 %all-to-all-start.7 = ((bf16[4,2,768,128]{3,2,1,0:T(8,128)(2,1)}), bf16[4,2,768,128]{3,2,1,0:T(8,128)(2,1)}, u32[]{:S(2)}, u32[]{:S(2)}) async-start(bf16[4,2,768,128]{3,2,1,0:T(8,128)(2,1)} %copy-done.8), calls=%async_computation.7 | async-start | bytes 3145728 | tf_op jit(solution)/shard_map/all_to_all | solution.py:278
  352.6 9.9 %collective-permute-start.15 = (bf16[512,256]{1,0:T(8,128)(2,1)S(1)}, bf16[512,256]{1,0:T(8,128)(2,1)S(1)}, u32[]{:S(2)}, u32[]{:S(2)}) collective-permute-start(bf16[512,256]{1,0:T(8,128)(2,1)S(1)} %pad_maximum_fusion), channel_id=1, source_target_pairs={{0,4},{4,0},{1,5},{5,1},{2,6},{6,2},{3,7},{7,3},{8,12},{12,8},{9,1... | collective-permute-start | bytes 786440 | tf_op jit(solution)/shard_map/ppermute | solution.py:274
  362.6 10.5 %collective-permute-start.16 = (bf16[512,256]{1,0:T(8,128)(2,1)S(1)}, bf16[512,256]{1,0:T(8,128)(2,1)S(1)}, u32[]{:S(2)}, u32[]{:S(2)}) collective-permute-start(bf16[512,256]{1,0:T(8,128)(2,1)S(1)} %multiply_convert_fusion.6.own), channel_id=1, source_target_pairs={{0,16},{1,17},{2,18},{3,19},{4,20},{5,21},{6,22},{7,23},{8,24},{9,... | collective-permute-start | bytes 786440 | tf_op jit(solution)/shard_map/ppermute | solution.py:350
  364.0 12.3 %collective-permute-start.17 = (bf16[512,256]{1,0:T(8,128)(2,1)S(1)}, bf16[512,256]{1,0:T(8,128)(2,1)S(1)}, u32[]{:S(2)}, u32[]{:S(2)}) collective-permute-start(bf16[512,256]{1,0:T(8,128)(2,1)S(1)} %multiply_convert_fusion.6.own), channel_id=1, source_target_pairs={{0,32},{1,33},{2,34},{3,35},{4,36},{5,37},{6,38},{7,39},{8,40},{9,... | collective-permute-start | bytes 786440 | tf_op jit(solution)/shard_map/ppermute | solution.py:350
  365.6 13.7 %collective-permute-start.18 = (bf16[512,256]{1,0:T(8,128)(2,1)S(1)}, bf16[512,256]{1,0:T(8,128)(2,1)S(1)}, u32[]{:S(2)}, u32[]{:S(2)}) collective-permute-start(bf16[512,256]{1,0:T(8,128)(2,1)S(1)} %multiply_convert_fusion.6.own), channel_id=1, source_target_pairs={{0,48},{1,49},{2,50},{3,51},{4,52},{5,53},{6,54},{7,55},{8,56},{9,... | collective-permute-start | bytes 786440 | tf_op jit(solution)/shard_map/ppermute | solution.py:350
  386.6 22.6 %all-to-all-start.1 = ((bf16[4,2,768,128]{3,2,1,0:T(8,128)(2,1)}), bf16[4,2,768,128]{3,2,1,0:T(8,128)(2,1)S(1)}, u32[]{:S(2)}, u32[]{:S(2)}) async-start(bf16[4,2,768,128]{3,2,1,0:T(8,128)(2,1)} %copy-done.9), calls=%async_computation.1 | async-start | bytes 3145728 | tf_op jit(solution)/shard_map/all_to_all | solution.py:278
  394.2 84.3 %collective-permute-start.40 = (bf16[768,512]{1,0:T(8,128)(2,1)}, bf16[768,512]{1,0:T(8,128)(2,1)}, u32[]{:S(2)}, u32[]{:S(2)}) collective-permute-start(bf16[768,512]{1,0:T(8,128)(2,1)} %get-tuple-element.20), channel_id=1, source_target_pairs={{0,64},{64,0},{1,65},{65,1},{2,66},{66,2},{3,67},{67,3},{4,68},{68... | collective-permute-start | bytes 2359304 | tf_op jit(solution)/shard_map/ppermute | solution.py:274
  399.7 95.6 %collective-permute-start.33 = (bf16[768,512]{1,0:T(8,128)(2,1)}, bf16[768,512]{1,0:T(8,128)(2,1)}, u32[]{:S(2)}, u32[]{:S(2)}) collective-permute-start(bf16[768,512]{1,0:T(8,128)(2,1)} %get-tuple-element.18), channel_id=1, source_target_pairs={{0,64},{64,0},{1,65},{65,1},{2,66},{66,2},{3,67},{67,3},{4,68},{68... | collective-permute-start | bytes 2359304 | tf_op jit(solution)/shard_map/ppermute | solution.py:274
  407.1 105.0 %collective-permute-start.26 = (bf16[768,512]{1,0:T(8,128)(2,1)}, bf16[768,512]{1,0:T(8,128)(2,1)}, u32[]{:S(2)}, u32[]{:S(2)}) collective-permute-start(bf16[768,512]{1,0:T(8,128)(2,1)} %get-tuple-element.16), channel_id=1, source_target_pairs={{0,64},{64,0},{1,65},{65,1},{2,66},{66,2},{3,67},{67,3},{4,68},{68... | collective-permute-start | bytes 2359304 | tf_op jit(solution)/shard_map/ppermute | solution.py:274
  409.6 119.2 %collective-permute-start.19 = (bf16[768,512]{1,0:T(8,128)(2,1)S(1)}, bf16[768,512]{1,0:T(8,128)(2,1)S(1)}, u32[]{:S(2)}, u32[]{:S(2)}) collective-permute-start(bf16[768,512]{1,0:T(8,128)(2,1)S(1)} %get-tuple-element.14), channel_id=1, source_target_pairs={{0,64},{64,0},{1,65},{65,1},{2,66},{66,2},{3,67},{67,3},{4,68},{68... | collective-permute-start | bytes 2359304 | tf_op jit(solution)/shard_map/ppermute | solution.py:274
  (28 other events, 343.0 us)
